TPU v7x, 64 devices: a 2x2x8 block of a 4x4x8 slice. The times are simulated.
64 devices in a mesh: req: 4 (over x, y), cp: 16 (over z, core).
Axes of the slice: x: 2, y: 2, z: 8, core: 2. Of those that a mesh axis runs over, the one named last changes fastest.
The devices are a block of a 4x4x8 slice.
Arguments:
- x: bfloat16 [16384, 2048], P(('req', 'cp')), parts along dimension 0
- token_ids: int32 [16], P('req'), parts along dimension 0
- embed_table: bfloat16 [49152, 2048], P('cp')
- norm_attn: bfloat16 [2, 2048], replicated
- w_q: bfloat16 [2, 2048, 32, 64], replicated
- w_k: bfloat16 [2, 2048, 32, 64], replicated
- w_v: bfloat16 [2, 2048, 32, 64], replicated
- w_o: bfloat16 [2, 32, 64, 2048], replicated
- norm_mlp: bfloat16 [2, 2048], replicated
- w_gate: bfloat16 [2, 2048, 8192], replicated
- w_up: bfloat16 [2, 2048, 8192], replicated
- w_down: bfloat16 [2, 8192, 2048], replicated
Outputs:
- output 1: bfloat16 [16384, 2048], P(('req', 'cp')), parts along dimension 0
- output 2: bfloat16 [2, 16384, 32, 64], P(None, 'req', 'cp'), parts along dimension 1
- output 3: bfloat16 [2, 16384, 32, 64], P(None, 'req', 'cp'), parts along dimension 1
- output 4: bfloat16 [16, 2048], P('req'), parts along dimension 0
There are 4 independent parts. A program takes and returns all parts, laid end to end along the dimension named above; an argument that names none is the same for every part.
All inputs are finite; a program needn't handle non-finite values.
Results may differ from a plain program's by a relative error of at most 0.0196713.
Values are sent between devices in bfloat16 or wider.
A program may use at most 768 MiB of HBM per device.

v0:
```python
import jax
import jax.numpy as jnp
from jax import lax
from jax.sharding import PartitionSpec as P

ROPE_BASE = 10000.0
NORM_EPS = 1e-5


def rms_norm(rows, gain_row):
    wide_rows = rows.astype(jnp.float32)
    inv_rms = lax.rsqrt(jnp.mean(wide_rows * wide_rows, axis=-1, keepdims=True) + NORM_EPS)
    return (wide_rows * inv_rms * gain_row.astype(jnp.float32)).astype(jnp.bfloat16)


def rope_tables(positions, head_dim):
    inv_freq = 1.0 / (ROPE_BASE ** (jnp.arange(0, head_dim, 2, dtype=jnp.float32) / head_dim))
    angles = positions.astype(jnp.float32)[..., None] * inv_freq
    return jnp.cos(angles), jnp.sin(angles)


def apply_rope(vectors, cos_tab, sin_tab):
    half_dim = vectors.shape[-1] // 2
    first = vectors[..., :half_dim]
    second = vectors[..., half_dim:]
    cosines = cos_tab[..., None, :]
    sines = sin_tab[..., None, :]
    return jnp.concatenate([first * cosines - second * sines, second * cosines + first * sines], axis=-1)


def stored_positions(device, group, seq_dev):
    block_len = seq_dev // 2
    offsets = jnp.arange(seq_dev, dtype=jnp.int32)
    return jnp.where(offsets < block_len, device * block_len + offsets, (2 * group - 1 - device) * block_len + offsets - block_len)


def to_natural(rows, group):
    block_len = rows.shape[1] // (2 * group)
    halves = rows.reshape((rows.shape[0], group, 2, block_len) + rows.shape[2:])
    ordered = jnp.concatenate([halves[:, :, 0], halves[:, ::-1, 1]], axis=1)
    return ordered.reshape((rows.shape[0], 2 * group * block_len) + rows.shape[2:])


def attend(queries, query_pos, keys, values, key_pos):
    num_rows, num_heads, head_dim = queries.shape
    kv_heads = keys.shape[1]
    grouped = queries.reshape(num_rows, kv_heads, num_heads // kv_heads, head_dim)
    scores = jnp.einsum('qhgd,khd->hgqk', grouped, keys, preferred_element_type=jnp.float32) * (head_dim ** -0.5)
    scores = jnp.where(query_pos[:, None] >= key_pos[None, :], scores, -jnp.inf)
    attn_probs = jax.nn.softmax(scores, axis=-1).astype(jnp.bfloat16)
    mixed = jnp.einsum('hgqk,khd->qhgd', attn_probs, values, preferred_element_type=jnp.float32)
    return mixed.astype(jnp.bfloat16).reshape(num_rows, num_heads, head_dim)


def mlp_block(hidden, gain_row, gate_weights, up_weights, down_weights):
    normed = rms_norm(hidden, gain_row)
    gate = jnp.dot(normed, gate_weights, preferred_element_type=jnp.float32)
    upward = jnp.dot(normed, up_weights, preferred_element_type=jnp.float32)
    gated = (jax.nn.silu(gate) * upward).astype(jnp.bfloat16)
    return (hidden.astype(jnp.float32) + jnp.dot(gated, down_weights, preferred_element_type=jnp.float32)).astype(jnp.bfloat16)


def solution(mesh):
    group = mesh.shape['cp']

    def local_program(x_rows, token_ids, table_rows, norm_attn, w_q, w_k, w_v, w_o, norm_mlp, w_gate, w_up, w_down):
        device = lax.axis_index('cp')
        num_layers, d_model, num_heads, head_dim = w_q.shape
        kv_heads = w_k.shape[2]
        ff_dim = w_gate.shape[2]
        seq_dev = x_rows.shape[0]
        seq_len = group * seq_dev
        steps = token_ids.shape[0]
        heads_dev = num_heads // group
        kv_dev = kv_heads // group
        ff_dev = ff_dim // group
        vocab_dev = table_rows.shape[0]
        my_pos = stored_positions(device, group, seq_dev)
        key_pos = stored_positions(jnp.arange(group, dtype=jnp.int32)[:, None], group, seq_dev).reshape(seq_len)
        cos_tab, sin_tab = rope_tables(my_pos, head_dim)
        hidden = x_rows
        k_saved = []
        v_saved = []
        for layer in range(num_layers):
            normed = rms_norm(hidden, norm_attn[layer])
            queries = apply_rope(jnp.einsum('sd,dhk->shk', normed, w_q[layer], preferred_element_type=jnp.float32), cos_tab, sin_tab).astype(jnp.bfloat16)
            keys = apply_rope(jnp.einsum('sd,dhk->shk', normed, w_k[layer], preferred_element_type=jnp.float32), cos_tab, sin_tab).astype(jnp.bfloat16)
            values = jnp.einsum('sd,dhk->shk', normed, w_v[layer], preferred_element_type=jnp.float32).astype(jnp.bfloat16)
            all_keys = lax.all_gather(keys, 'cp', axis=0, tiled=True)
            all_values = lax.all_gather(values, 'cp', axis=0, tiled=True)
            mixed = attend(queries, my_pos, all_keys, all_values, key_pos)
            attn_out = jnp.einsum('shk,hkm->sm', mixed, w_o[layer], preferred_element_type=jnp.float32)
            hidden = (hidden.astype(jnp.float32) + attn_out).astype(jnp.bfloat16)
            hidden = mlp_block(hidden, norm_mlp[layer], w_gate[layer], w_up[layer], w_down[layer])
            k_saved.append(keys)
            v_saved.append(values)
        k_heads = lax.all_to_all(jnp.stack(k_saved), 'cp', 2, 1, tiled=True)
        v_heads = lax.all_to_all(jnp.stack(v_saved), 'cp', 2, 1, tiled=True)
        k_cache = to_natural(k_heads, group)
        v_cache = to_natural(v_heads, group)
        local_ids = token_ids - device * vocab_dev
        in_range = (local_ids >= 0) & (local_ids < vocab_dev)
        picked = jnp.take(table_rows, jnp.clip(local_ids, 0, vocab_dev - 1), axis=0)
        dec_hidden = lax.psum(jnp.where(in_range[:, None], picked, jnp.zeros_like(picked)), 'cp')
        dec_pos = seq_len + jnp.arange(steps, dtype=jnp.int32)
        all_pos = jnp.concatenate([jnp.arange(seq_len, dtype=jnp.int32), dec_pos])
        dec_cos, dec_sin = rope_tables(dec_pos, head_dim)
        for layer in range(num_layers):
            q_weights = lax.dynamic_index_in_dim(w_q[layer].reshape(d_model, group, heads_dev, head_dim), device, axis=1, keepdims=False)
            k_weights = lax.dynamic_index_in_dim(w_k[layer].reshape(d_model, group, kv_dev, head_dim), device, axis=1, keepdims=False)
            v_weights = lax.dynamic_index_in_dim(w_v[layer].reshape(d_model, group, kv_dev, head_dim), device, axis=1, keepdims=False)
            o_weights = lax.dynamic_index_in_dim(w_o[layer].reshape(group, heads_dev, head_dim, d_model), device, axis=0, keepdims=False)
            normed = rms_norm(dec_hidden, norm_attn[layer])
            queries = apply_rope(jnp.einsum('td,dhk->thk', normed, q_weights, preferred_element_type=jnp.float32), dec_cos, dec_sin).astype(jnp.bfloat16)
            new_keys = apply_rope(jnp.einsum('td,dhk->thk', normed, k_weights, preferred_element_type=jnp.float32), dec_cos, dec_sin).astype(jnp.bfloat16)
            new_values = jnp.einsum('td,dhk->thk', normed, v_weights, preferred_element_type=jnp.float32).astype(jnp.bfloat16)
            keys = jnp.concatenate([k_cache[layer], new_keys], axis=0)
            values = jnp.concatenate([v_cache[layer], new_values], axis=0)
            mixed = attend(queries, dec_pos, keys, values, all_pos)
            partial = jnp.einsum('thk,hkm->tm', mixed, o_weights, preferred_element_type=jnp.float32)
            dec_hidden = (dec_hidden.astype(jnp.float32) + lax.psum(partial, 'cp')).astype(jnp.bfloat16)
            gate_weights = lax.dynamic_index_in_dim(w_gate[layer].reshape(d_model, group, ff_dev), device, axis=1, keepdims=False)
            up_weights = lax.dynamic_index_in_dim(w_up[layer].reshape(d_model, group, ff_dev), device, axis=1, keepdims=False)
            down_weights = lax.dynamic_index_in_dim(w_down[layer].reshape(group, ff_dev, d_model), device, axis=0, keepdims=False)
            normed = rms_norm(dec_hidden, norm_mlp[layer])
            gate = jnp.dot(normed, gate_weights, preferred_element_type=jnp.float32)
            upward = jnp.dot(normed, up_weights, preferred_element_type=jnp.float32)
            gated = (jax.nn.silu(gate) * upward).astype(jnp.bfloat16)
            partial = jnp.dot(gated, down_weights, preferred_element_type=jnp.float32)
            dec_hidden = (dec_hidden.astype(jnp.float32) + lax.psum(partial, 'cp')).astype(jnp.bfloat16)
        return hidden, k_cache, v_cache, dec_hidden

    replicated = P()
    in_specs = (P(('req', 'cp'), None), P('req'), P('cp', None), replicated, replicated, replicated, replicated, replicated, replicated, replicated, replicated, replicated)
    out_specs = (P(('req', 'cp'), None), P(None, 'req', 'cp', None), P(None, 'req', 'cp', None), P('req', None))
    return jax.shard_map(local_program, mesh=mesh, in_specs=in_specs, out_specs=out_specs, check_vma=False)
```

profile of v0, /device:TPU:23, one launch (start us, length us, event | category | flops | bytes accessed | tf_op | source)
XLA Modules:
  0.0 1259.5 jit_solution(6203491542659518629)
XLA Ops:
  56.8 83.4 %all-gather.7.cloned.1.call-done = bf16[4096,32,64]{0,2,1:T(8,128)(2,1)} async-done(((bf16[256,32,64]{0,2,1:T(8,128)(2,1)}), bf16[4096,32,64]{0,2,1:T(8,128)(2,1)}) %all-gather.7.cloned.1.call-update) | async-done | bytes 16777232 | tf_op jit(solution)/shard_map/all_gather | solution.py:89
  140.2 52.2 %fusion.2 = (f32[32,256]{1,0:T(8,128)S(1)}, f32[32,4096,256]{2,1,0:T(8,128)}) fusion(pred[256,4096]{0,1:T(8,128)(4,1)S(1)} %broadcast_compare_fusion, bf16[4096,32,64]{0,2,1:T(8,128)(2,1)} %all-gather.7.cloned.1.call-done, bf16[256,32,32]{0,2,1:T(8,128)(2,1)S(1)} %get-tuple-element.31, bf16[256,32,32]{0,2,1:T(8,128)(2,1)S(1)} %get-tuple-element.30), kind=kOutput, calls=%fused_computation.9 | convolution fusion | flops 4397719552 | bytes 153124864 | tf_op jit(solution)/shard_map/qhgd,khd->hgqk/dot_general | solution.py:48
  192.4 41.1 %fusion = f32[32,256]{1,0:T(8,128)S(1)} fusion(f32[32,4096,256]{2,1,0:T(8,128)} %get-tuple-element.68, f32[32,256]{1,0:T(8,128)S(1)} %get-tuple-element.67, pred[256,4096]{0,1:T(8,128)(4,1)S(1)} %broadcast_compare_fusion), kind=kLoop, calls=%fused_computation.7 | loop fusion | flops 134209536 | bytes 135331840 | tf_op jit(solution)/shard_map/reduce_sum | solution.py:50
  238.0 49.8 %fusion.127 = bf16[256,32,64]{0,2,1:T(8,128)(2,1)S(1)} fusion(bf16[4096,32,64]{0,2,1:T(8,128)(2,1)} %all-gather.5.cloned.1.call-done, f32[32,256]{1,0:T(8,128)S(1)} %fusion, f32[32,256]{1,0:T(8,128)S(1)} %get-tuple-element.67, f32[32,4096,256]{2,1,0:T(8,128)} %get-tuple-element.68, pred[256,4096]{0,1:T(8,128)(4,1)S(1)} %broadcast_compare_fusion), kind=kOutput, calls=%fused_computation.121 | convolution fusion | flops 4463263744 | bytes 153157632 | tf_op jit(solution)/shard_map/hgqk,khd->qhgd/dot_general | solution.py:51
  293.7 17.3 %fusion.14 = f32[256,8192]{1,0:T(8,128)} fusion(bf16[256,2048]{1,0:T(8,128)(2,1)S(1)} %get-tuple-element.70, f32[2048]{0:T(1024)S(1)} %bitcast.453, f32[256]{0:T(256)S(1)} %add_rsqrt_fusion.2, bf16[2,2048,8192]{2,1,0:T(8,128)(2,1)} %param.21), kind=kOutput, calls=%fused_computation.21 | convolution fusion | flops 8592031744 | bytes 43000832 | tf_op jit(solution)/shard_map/dot_general | solution.py:57
  311.0 18.6 %fusion.29.clone.5.clone.5 = bf16[256,8192]{1,0:T(8,128)(2,1)} fusion(f32[256,8192]{1,0:T(8,128)} %fusion.14, bf16[256,2048]{1,0:T(8,128)(2,1)S(1)} %get-tuple-element.70, f32[2048]{0:T(1024)S(1)} %bitcast.454, f32[256]{0:T(256)S(1)} %add_rsqrt_fusion.2, bf16[2,2048,8192]{2,1,0:T(8,128)(2,1)} %param.22), kind=kOutput, calls=%fused_computation.30.clone.clone.clone.clone.clone.clone.clone.clone.clone.2 | convolution fusion | flops 8604614656 | bytes 47195136 | tf_op jit(solution)/shard_map/dot_general | solution.py:58
  369.1 47.1 %psum.35 = bf16[4,2048]{1,0:T(4,128)(2,1)S(1)} all-reduce(bf16[4,2048]{1,0:T(4,128)(2,1)S(1)} %select_select_fusion), channel_id=1, replica_groups=mesh['req'=4,'cp'=16] {'cp'}, use_global_device_ids=true, to_apply=%region_8.9 | all-reduce | flops 8192 | bytes 32768 | tf_op jit(solution)/shard_map/psum | solution.py:104
  420.2 44.5 %fusion.328 = (bf16[1,2048,8192]{2,1,0:T(8,128)(2,1)}, bf16[1,2048,8192]{2,1,0:T(8,128)(2,1)}) fusion(bf16[2,2048,8192]{2,1,0:T(8,128)(2,1)} %param.21), kind=kLoop, calls=%fused_computation.340 | loop fusion | bytes 134217728 | tf_op jit(solution)/shard_map/slice | solution.py:94
  464.7 44.5 %fusion.329 = (bf16[1,2048,8192]{2,1,0:T(8,128)(2,1)}, bf16[1,2048,8192]{2,1,0:T(8,128)(2,1)}) fusion(bf16[2,2048,8192]{2,1,0:T(8,128)(2,1)} %param.22), kind=kLoop, calls=%fused_computation.341 | loop fusion | bytes 134217728 | tf_op jit(solution)/shard_map/slice | solution.py:94
  527.6 43.5 %fusion.330 = (bf16[1,8192,2048]{2,1,0:T(8,128)(2,1)}, bf16[1,8192,2048]{2,1,0:T(8,128)(2,1)}) fusion(bf16[2,8192,2048]{2,1,0:T(8,128)(2,1)} %param.23), kind=kLoop, calls=%fused_computation.342 | loop fusion | bytes 134217728 | tf_op jit(solution)/shard_map/slice | solution.py:94
  573.0 20.5 %all-to-all-done = bf16[2,256,32,64]{1,3,0,2:T(8,128)(2,1)} async-done(((bf16[2,256,32,64]{1,3,0,2:T(8,128)(2,1)}), bf16[2,256,32,64]{1,3,0,2:T(8,128)(2,1)}, u32[]{:S(2)}, u32[]{:S(2)}) %all-to-all-start) | async-done | bytes 2097184 | tf_op jit(solution)/shard_map/all_to_all | solution.py:97
  602.3 44.4 %copy.144 = bf16[1,2048,8192]{1,2,0:T(8,128)(2,1)} copy(bf16[1,2048,8192]{2,1,0:T(8,128)(2,1)} %get-tuple-element.12) | data formatting | bytes 67108864
  646.8 44.4 %copy.145 = bf16[1,2048,8192]{1,2,0:T(8,128)(2,1)} copy(bf16[1,2048,8192]{2,1,0:T(8,128)(2,1)} %get-tuple-element.14) | data formatting | bytes 67108864
  691.2 44.3 %copy.146 = bf16[1,2048,8192]{1,2,0:T(8,128)(2,1)} copy(bf16[1,2048,8192]{2,1,0:T(8,128)(2,1)} %get-tuple-element.13) | data formatting | bytes 67108864
  735.5 44.5 %copy.147 = bf16[1,2048,8192]{1,2,0:T(8,128)(2,1)} copy(bf16[1,2048,8192]{2,1,0:T(8,128)(2,1)} %get-tuple-element.15) | data formatting | bytes 67108864
  837.8 45.0 %psum.36 = f32[4,2048]{1,0:T(4,128)S(1)} all-reduce(f32[4,2048]{1,0:T(4,128)S(1)} %convolution_bitcast_fusion.1), channel_id=1, replica_groups=mesh['req'=4,'cp'=16] {'cp'}, use_global_device_ids=true, to_apply=%region_12.13 | all-reduce | flops 8192 | bytes 65536 | tf_op jit(solution)/shard_map/psum | solution.py:121
  888.4 45.9 %psum.37 = f32[4,2048]{1,0:T(4,128)S(1)} all-reduce(f32[4,2048]{1,0:T(4,128)S(1)} %fusion.110), channel_id=1, replica_groups=mesh['req'=4,'cp'=16] {'cp'}, use_global_device_ids=true, to_apply=%region_14.15 | all-reduce | flops 8192 | bytes 65536 | tf_op jit(solution)/shard_map/psum | solution.py:130
  948.2 45.8 %psum.38 = f32[4,2048]{1,0:T(4,128)S(1)} all-reduce(f32[4,2048]{1,0:T(4,128)S(1)} %convolution_bitcast_fusion), channel_id=1, replica_groups=mesh['req'=4,'cp'=16] {'cp'}, use_global_device_ids=true, to_apply=%region_18.19 | all-reduce | flops 8192 | bytes 65536 | tf_op jit(solution)/shard_map/psum | solution.py:121
  999.6 46.0 %psum.39 = f32[4,2048]{1,0:T(4,128)S(1)} all-reduce(f32[4,2048]{1,0:T(4,128)S(1)} %fusion.108), channel_id=1, replica_groups=mesh['req'=4,'cp'=16] {'cp'}, use_global_device_ids=true, to_apply=%region_20.21 | all-reduce | flops 8192 | bytes 65536 | tf_op jit(solution)/shard_map/psum | solution.py:130
  1051.0 51.6 %fusion.3 = (f32[32,256]{1,0:T(8,128)S(1)}, f32[32,4096,256]{2,1,0:T(8,128)}) fusion(pred[256,4096]{0,1:T(8,128)(4,1)S(1)} %copy-done.1, bf16[4096,32,64]{0,2,1:T(8,128)(2,1)} %all-gather.11.cloned.1.call-done, bf16[256,32,32]{0,2,1:T(8,128)(2,1)} %get-tuple-element.27, bf16[256,32,32]{0,2,1:T(8,128)(2,1)} %get-tuple-element.26), kind=kOutput, calls=%fused_computation.10 | convolution fusion | flops 4397719552 | bytes 153124864 | tf_op jit(solution)/shard_map/qhgd,khd->hgqk/dot_general | solution.py:48
  1102.7 41.1 %fusion.1 = f32[32,256]{1,0:T(8,128)S(1)} fusion(f32[32,4096,256]{2,1,0:T(8,128)} %get-tuple-element.74, f32[32,256]{1,0:T(8,128)S(1)} %get-tuple-element.73, pred[256,4096]{0,1:T(8,128)(4,1)S(1)} %copy-done.1), kind=kLoop, calls=%fused_computation.8 | loop fusion | flops 134209536 | bytes 135331840 | tf_op jit(solution)/shard_map/reduce_sum | solution.py:50
  1143.8 49.8 %fusion.124 = bf16[256,32,64]{0,2,1:T(8,128)(2,1)S(1)} fusion(bf16[4096,32,64]{0,2,1:T(8,128)(2,1)} %all-gather.9.cloned.1.call-done, f32[32,256]{1,0:T(8,128)S(1)} %fusion.1, f32[32,256]{1,0:T(8,128)S(1)} %get-tuple-element.73, f32[32,4096,256]{2,1,0:T(8,128)} %get-tuple-element.74, pred[256,4096]{0,1:T(8,128)(4,1)S(1)} %copy-done.1), kind=kOutput, calls=%fused_computation.120 | convolution fusion | flops 4463263744 | bytes 153157632 | tf_op jit(solution)/shard_map/hgqk,khd->qhgd/dot_general | solution.py:51
  1199.5 17.4 %fusion.10 = f32[256,8192]{1,0:T(8,128)} fusion(bf16[256,2048]{1,0:T(8,128)(2,1)S(1)} %get-tuple-element.76, f32[2048]{0:T(1024)S(1)} %bitcast.451, f32[256]{0:T(256)S(1)} %add_rsqrt_fusion, bf16[2,2048,8192]{2,1,0:T(8,128)(2,1)} %param.21), kind=kOutput, calls=%fused_computation.17 | convolution fusion | flops 8592031744 | bytes 43000832 | tf_op jit(solution)/shard_map/dot_general | solution.py:57
  1216.9 18.5 %fusion.26.clone.9 = bf16[256,8192]{1,0:T(8,128)(2,1)} fusion(f32[256,8192]{1,0:T(8,128)} %fusion.10, bf16[256,2048]{1,0:T(8,128)(2,1)S(1)} %get-tuple-element.76, f32[2048]{0:T(1024)S(1)} %bitcast.452, f32[256]{0:T(256)S(1)} %add_rsqrt_fusion, bf16[2,2048,8192]{2,1,0:T(8,128)(2,1)} %param.22), kind=kOutput, calls=%fused_computation.29.clone.clone.clone.clone.clone.clone.clone.2 | convolution fusion | flops 8604614656 | bytes 47195136 | tf_op jit(solution)/shard_map/dot_general | solution.py:58
  (210 shorter events, 243.3 us)
Async XLA Ops:
  7.2 133.0 %all-gather.7.cloned.1.call-start = ((), (), s32[]{:S(2)}) async-start(), calls=%async_computation.3 | async-start | bytes 17825792 | tf_op jit(solution)/shard_map/all_gather | solution.py:89
  7.3 27.8 %copy-start.34 = (f32[32]{0:T(128)}, f32[32]{0:T(128)S(1)}, u32[]{:S(2)}) copy-start(f32[32]{0:T(128)S(1)} %negate_power_fusion) | copy-start | bytes 388
  7.3 12.4 slice-start
  8.8 39.1 %copy-start.27 = (f32[1,2048]{1,0:T(1,128)}, f32[1,2048]{1,0:T(1,128)S(1)}, u32[]{:S(2)}) copy-start(f32[1,2048]{1,0:T(1,128)S(1)} %get-tuple-element.57) | copy-start | bytes 24580
  8.8 16.0 %slice-start.3 = ((s8[16777216]{0:T(1024)(128)(4,1)}), s8[4194304]{0:T(1024)(128)(4,1)S(1)}, s32[]{:S(2)}) async-start(s8[16777216]{0:T(1024)(128)(4,1)} %bitcast.399), calls=%async_computation.9 | async-start | bytes 8388608
  38.1 199.9 %all-gather.5.cloned.1.call-start = ((), (), s32[]{:S(2)}) async-start(), calls=%async_computation.2 | async-start | bytes 17825792 | tf_op jit(solution)/shard_map/all_gather | solution.py:90
  53.6 997.4 %all-gather.11.cloned.1.call-start = ((), (), s32[]{:S(2)}) async-start(), calls=%async_computation.5 | async-start | bytes 17825792 | tf_op jit(solution)/shard_map/all_gather | solution.py:89
  56.7 181.2 %copy-start = (pred[256,4096]{0,1:T(8,128)(4,1)}, pred[256,4096]{0,1:T(8,128)(4,1)S(1)}, u32[]{:S(2)}) copy-start(pred[256,4096]{0,1:T(8,128)(4,1)S(1)} %broadcast_compare_fusion) | copy-start | bytes 3145732
  238.0 49.8 %copy-start.20 = (bf16[256,2048]{1,0:T(8,128)(2,1)S(1)}, bf16[256,2048]{1,0:T(8,128)(2,1)}, u32[]{:S(2)}) copy-start(bf16[256,2048]{1,0:T(8,128)(2,1)} %param.12) | copy-start | bytes 3145732
  329.5 16.6 %copy-start.25 = (f32[1,2048]{1,0:T(1,128)S(1)}, f32[1,2048]{1,0:T(1,128)}, u32[]{:S(2)}) copy-start(f32[1,2048]{1,0:T(1,128)} %get-tuple-element.56) | copy-start | bytes 24580
  358.3 58.1 %copy-start.28 = (f32[1,2048]{1,0:T(1,128)S(1)}, f32[1,2048]{1,0:T(1,128)}, u32[]{:S(2)}) copy-start(f32[1,2048]{1,0:T(1,128)} %copy-done.27) | copy-start | bytes 24580
  358.3 60.8 %copy-start.10 = (f32[256,2048]{0,1:S(1)}, f32[256,2048]{0,1}, u32[]{:S(2)}) copy-start(f32[256,2048]{0,1} %copy-done.9) | copy-start | bytes 6291460
  362.1 781.7 %all-gather.9.cloned.1.call-start = ((), (), s32[]{:S(2)}) async-start(), calls=%async_computation.4 | async-start | bytes 17825792 | tf_op jit(solution)/shard_map/all_gather | solution.py:90
  519.7 73.8 %all-to-all-start = ((bf16[2,256,32,64]{1,3,0,2:T(8,128)(2,1)}), bf16[2,256,32,64]{1,3,0,2:T(8,128)(2,1)}, u32[]{:S(2)}, u32[]{:S(2)}) async-start(bf16[2,256,32,64]{1,3,0,2:T(8,128)(2,1)} %copy.120), calls=%async_computation | async-start | bytes 4194304 | tf_op jit(solution)/shard_map/all_to_all | solution.py:97
  527.6 43.7 %copy-start.17 = (bf16[1,256,32,64]{1,3,2,0:T(8,128)(2,1)S(1)}, bf16[1,256,32,64]{1,3,2,0:T(8,128)(2,1)}, u32[]{:S(2)}) copy-start(bf16[1,256,32,64]{1,3,2,0:T(8,128)(2,1)} %convert_bitcast_fusion) | copy-start | bytes 3145732
  571.2 29.3 %copy-start.35 = (f32[32]{0:T(128)S(1)}, f32[32]{0:T(128)}, u32[]{:S(2)}) copy-start(f32[32]{0:T(128)} %copy-done.34) | copy-start | bytes 388
  593.5 219.5 %all-to-all-start.1 = ((bf16[2,256,32,64]{1,3,0,2:T(8,128)(2,1)}), bf16[2,256,32,64]{1,3,0,2:T(8,128)(2,1)}, u32[]{:S(2)}, u32[]{:S(2)}) async-start(bf16[2,256,32,64]{1,3,0,2:T(8,128)(2,1)} %copy.123), calls=%async_computation.1 | async-start | bytes 4194304 | tf_op jit(solution)/shard_map/all_to_all | solution.py:98
  828.3 54.7 %copy-start.32 = (f32[1,2048]{1,0:T(1,128)S(1)}, f32[1,2048]{1,0:T(1,128)}, u32[]{:S(2)}) copy-start(f32[1,2048]{1,0:T(1,128)} %get-tuple-element.55) | copy-start | bytes 24580
  831.8 102.7 %copy-start.26 = (f32[1,2048]{1,0:T(1,128)S(1)}, f32[1,2048]{1,0:T(1,128)}, u32[]{:S(2)}) copy-start(f32[1,2048]{1,0:T(1,128)} %get-tuple-element.56) | copy-start | bytes 24580
  831.8 105.7 %copy-start.18 = (bf16[1,32,128,2,64]{2,4,3,1,0:T(8,128)(2,1)S(1)}, bf16[1,32,128,2,64]{2,4,3,1,0:T(8,128)(2,1)}, u32[]{:S(2)}) copy-start(bf16[1,32,128,2,64]{2,4,3,1,0:T(8,128)(2,1)} %get-tuple-element.34) | copy-start | bytes 3145732
  888.4 105.7 %copy-start.29 = (f32[1,2048]{1,0:T(1,128)S(1)}, f32[1,2048]{1,0:T(1,128)}, u32[]{:S(2)}) copy-start(f32[1,2048]{1,0:T(1,128)} %get-tuple-element.54) | copy-start | bytes 24580
  944.2 105.2 %copy-start.6 = (bf16[2,16,1,128,2,64]{3,5,2,4,1,0:T(8,128)(2,1)S(1)}, bf16[2,16,1,128,2,64]{3,5,2,4,1,0:T(8,128)(2,1)}, u32[]{:S(2)}) copy-start(bf16[2,16,1,128,2,64]{3,5,2,4,1,0:T(8,128)(2,1)} %copy-done.5) | copy-start | bytes 3145732
  946.1 105.0 %copy-start.1 = (pred[256,4096]{0,1:T(8,128)(4,1)S(1)}, pred[256,4096]{0,1:T(8,128)(4,1)}, u32[]{:S(2)}) copy-start(pred[256,4096]{0,1:T(8,128)(4,1)} %copy-done) | copy-start | bytes 3145732
  1143.8 49.8 %copy-start.38 = (bf16[256,2048]{1,0:T(8,128)(2,1)S(1)}, bf16[256,2048]{1,0:T(8,128)(2,1)}, u32[]{:S(2)}) copy-start(bf16[256,2048]{1,0:T(8,128)(2,1)} %copy-done.37) | copy-start | bytes 3145732
  (25 other events, 115.8 us)
Sparse Core Ops, SparseCore 0:
  38.2 101.9 all-gather.6
  142.3 95.6 all-gather.4
  362.2 96.3 all-gather.10
  516.8 188.1 all-gather.8
where the time goes:
time: 1280 us; the launch traced here: 1260 us
  local copies, waits for them, and re-layouts  411 us (32%)
  matrix products  373 us (29%)
  blocking collectives  230 us (18%)
  waiting for transfers between devices  109 us (9%)
  other arithmetic  106 us (8%)
  starting transfers between devices  15.5 us (1%)
  between operations  15 us (1%)
    unnamed x95, local copies, waits for them, and re-layouts  193 us
    psum x4, blocking collectives, local_program(): lax.psum(partial, 'cp')  183 us
    dot_general x4, matrix products, attend(): jnp.einsum('qhgd,khd->hgqk', grouped, keys, preferred_element_type=jnp.fl...  107 us
    dot_general x2, matrix products, attend(): jnp.einsum('hgqk,khd->qhgd', attn_probs, values, preferred_element_type=j...  99.6 us
    all_gather x2, waiting for transfers between devices, local_program(): all_keys = lax.all_gather(keys, 'cp', axis=0, tiled=True)  83.4 us
    reduce_sum x4, other arithmetic, attend(): attn_probs = jax.nn.softmax(scores, axis=-1).astype(jnp.bfloat16)  82.6 us
    psum x1, blocking collectives, local_program(): lax.psum(jnp.where(in_range[:, None], picked, jnp.zeros_like(picked)), 'cp')  47.1 us
    slice x1, local copies, waits for them, and re-layouts, local_program(): w_up[layer]  44.5 us
  transfers between devices with their start and end apart: 6, of which 3 were waited for; matrix products, arithmetic and copies ran while one was open for 50% of the time, Pallas kernels for 0%

commit v1 on v0

v1 whole, which is shorter than its diff:
```python
import functools

import jax
import jax.numpy as jnp
from jax import lax
from jax.experimental import pallas as pl
from jax.experimental.pallas import tpu as pltpu
from jax.sharding import PartitionSpec as P

ROPE_BASE = 10000.0
NORM_EPS = 1e-5
LOG2_E = 1.4426950408889634
BF16 = jnp.bfloat16
F32 = jnp.float32
MESH = pl.DeviceIdType.MESH
LANES = 128
PAD = 16
QKV_ROWS = 512
FF_TILE = 512
FF_SLOTS = 3
KEY_TILE = 512
SPLIT = 11


def pick_kernel(vocab_dev, ids_ref, base_ref, table_ref, out_ref, rows, sems):
    steps = ids_ref.shape[0]
    base = base_ref[0]

    def copy(t):
        local = jnp.clip(ids_ref[t] - base, 0, vocab_dev - 1)
        start = pl.multiple_of((local // 8) * 8, 8)
        return pltpu.make_async_copy(table_ref.at[pl.ds(start, 8), :], rows.at[t], sems.at[t])

    for t in range(steps):
        copy(t).start()
    out_ref[...] = jnp.zeros_like(out_ref)
    picked = []
    for t in range(steps):
        copy(t).wait()
        local = ids_ref[t] - base
        inside = (local >= 0) & (local < vocab_dev)
        which = jnp.where(inside, lax.rem(jnp.clip(local, 0, vocab_dev - 1), 8), -1)
        index = lax.broadcasted_iota(jnp.int32, rows.shape[1:], 0)
        picked.append(jnp.sum(jnp.where(index == which, rows[t].astype(F32), 0.0), axis=0, keepdims=True))
    picked.append(jnp.zeros((PAD - steps, rows.shape[2]), F32))
    out_ref[...] = jnp.concatenate(picked, axis=0).astype(BF16)


def pick_rows(token_ids, base, table_rows):
    vocab_dev, d_model = table_rows.shape
    steps = token_ids.shape[0]
    return pl.pallas_call(
        functools.partial(pick_kernel, vocab_dev),
        out_shape=jax.ShapeDtypeStruct((PAD, d_model), BF16),
        in_specs=[
            pl.BlockSpec(memory_space=pltpu.SMEM),
            pl.BlockSpec(memory_space=pltpu.SMEM),
            pl.BlockSpec(memory_space=pl.ANY),
        ],
        out_specs=pl.BlockSpec(memory_space=pltpu.VMEM),
        scratch_shapes=[pltpu.VMEM((steps, 8, d_model), BF16), pltpu.SemaphoreType.DMA((steps,))],
        name="pick_rows",
    )(token_ids, base, table_rows)


def main_kernel(
    group, head_dim, num_layers, steps,
    x_in, emb_in, gain_attn, gain_mlp, tables, w_q, w_k, w_v, w_o, w_gate, w_up, w_down,
    x_out, k_cache, v_cache, dec_out,
    rows_x, rows_h, mixed, sent, got, key_rows, mixed_sent, score, best, run_max, run_acc,
    qkv_ring, wo_buf, gate_ring, up_ring, down_ring, dec_w, dec_h, dec_q, dec_k, dec_v, acc, gated, emb_part, emb_full, emb_sum, dec_sent,
    sem_x, sem_qkv, sem_wo, sem_ff, sem_dec, send_qkv, recv_qkv, send_o, recv_o, send_d, recv_d, send_e, recv_e, send_f, recv_f, sem_cache, sem_out,
):
    me = lax.axis_index("cp")
    blk = LANES
    blocks = 2 * group
    d_model = rows_x.shape[1]
    ff_dim = w_gate.shape[1]
    ff_steps = ff_dim // FF_TILE
    heads_dev = LANES // head_dim
    per_tile = QKV_ROWS // LANES
    tiles = d_model // QKV_ROWS
    half = head_dim // 2
    pair_blocks = KEY_TILE // blk
    pairs = group // pair_blocks
    exp_scale = float(head_dim ** -0.5 * LOG2_E)
    acc_rows = run_acc.shape[2]
    last = num_layers - 1
    b_rows = blk + PAD
    others = group - 1
    neighbour = lax.rem(me + 1, group)
    w_qkv = (w_q, w_k, w_v)
    order_a = (1, 2, 0)

    def remote(src, dst, ssem, rsem, device):
        return pltpu.make_async_remote_copy(src_ref=src, dst_ref=dst, send_sem=ssem, recv_sem=rsem, device_id={"cp": device}, device_id_type=MESH)

    def wait_recv(ref, sem):
        remote(ref, ref, send_e, sem, neighbour).wait_recv()

    def wait_send(ref, sem):
        remote(ref, ref, sem, recv_e, neighbour).wait_send()

    def tile_of(r):
        return lax.rem(r + me // per_tile + 1, tiles)

    def qkv_copy(layer, tensor, r):
        start = pl.multiple_of(layer * d_model + tile_of(r) * QKV_ROWS, QKV_ROWS)
        return pltpu.make_async_copy(w_qkv[tensor].at[pl.ds(start, QKV_ROWS), :], qkv_ring.at[r], sem_qkv.at[r])

    def wo_copy(layer, n):
        start = pl.multiple_of(layer * d_model, d_model)
        return pltpu.make_async_copy(w_o.at[pl.ds(start, d_model), pl.ds(n * QKV_ROWS, QKV_ROWS)], wo_buf.at[n], sem_wo.at[n])

    def gu_copies(layer, step):
        slot = lax.rem(step, FF_SLOTS)
        start = pl.multiple_of(layer * d_model, d_model)
        col = pl.multiple_of(step * FF_TILE, FF_TILE)
        return (
            pltpu.make_async_copy(w_gate.at[pl.ds(start, d_model), pl.ds(col, FF_TILE)], gate_ring.at[slot], sem_ff.at[0, slot]),
            pltpu.make_async_copy(w_up.at[pl.ds(start, d_model), pl.ds(col, FF_TILE)], up_ring.at[slot], sem_ff.at[1, slot]),
        )

    def down_copy(layer, step):
        slot = lax.rem(step, FF_SLOTS)
        start = pl.multiple_of(layer * ff_dim + step * FF_TILE, FF_TILE)
        return pltpu.make_async_copy(w_down.at[pl.ds(start, FF_TILE), :], down_ring.at[slot], sem_ff.at[2, slot])

    def dec_copy(layer, tensor):
        start = pl.multiple_of(layer * d_model + me * LANES, LANES)
        return pltpu.make_async_copy(w_qkv[tensor].at[pl.ds(start, LANES), :], dec_w.at[tensor], sem_dec.at[tensor])

    def block_of(chunk, device):
        return device if chunk == 0 else blocks - 1 - device

    def qkv_piece(layer, tensor, chunk, device):
        return remote(
            sent.at[tensor, chunk, device], got.at[layer, tensor, block_of(chunk, me)],
            send_qkv.at[chunk, tensor], recv_qkv.at[layer, chunk, tensor], device,
        )

    def send_to(piece, device):
        @pl.when(device != me)
        def _():
            piece.start()

    def send_all(layer, tensor, chunk):
        def body(i, carry):
            device = lax.rem(me + 1 + i, group)
            qkv_piece(layer, tensor, chunk, device).start()
            return carry

        lax.fori_loop(0, others, body, 0)

    def normalize(read, row0, count, gain):
        part = 64 if count % 64 == 0 else 48

        def body(i, carry):
            rows = pl.ds(pl.multiple_of(i * part, 16), part)
            wide = read(rows)
            inv = lax.rsqrt(jnp.mean(wide * wide, axis=-1, keepdims=True) + NORM_EPS)
            rows_h[pl.ds(pl.multiple_of(row0 + i * part, 16), part), :] = (wide * inv * gain).astype(BF16)
            return carry

        lax.fori_loop(0, count // part, body, 0)

    def normalize_x(row0, count, gain):
        def read(rows):
            return rows_x[pl.ds(pl.multiple_of(row0 + rows.start, 16), rows.size), :].astype(F32)

        normalize(read, row0, count, gain)

    def rotate(flat, which):
        cosines, sines = tables[2 * which], tables[2 * which + 1]
        heads = flat.reshape(flat.shape[0] // head_dim, head_dim, flat.shape[1])
        first, second = heads[:, :half], heads[:, half:]
        turned = jnp.concatenate([first * cosines - second * sines, second * cosines + first * sines], axis=1)
        return turned.reshape(flat.shape)

    def project(layer, chunk):
        order = order_a if chunk == 0 else order_a[::-1]
        for place, tensor in enumerate(order):
            def body(r, carry, place=place, tensor=tensor):
                if chunk == 0 or place > 0:
                    qkv_copy(layer, tensor, r).wait()
                flat = lax.dot_general(
                    qkv_ring[r], rows_h[chunk * blk:(chunk + 1) * blk, :], (((1,), (1,)), ((), ())), preferred_element_type=F32
                )
                if tensor != 2:
                    flat = rotate(flat, chunk)
                first = tile_of(r) * per_tile
                sent[tensor, chunk, pl.ds(first, per_tile)] = flat.astype(BF16).reshape(per_tile, LANES, blk)
                if chunk == 0 or tensor == 0:
                    for i in range(per_tile):
                        send_to(qkv_piece(layer, tensor, chunk, first + i), first + i)
                if place < 2:
                    qkv_copy(layer, order[place + 1], r).start()
                elif chunk == 1:
                    @pl.when(layer < last)
                    def _():
                        qkv_copy(layer + 1, order_a[0], r).start()
                return carry

            lax.fori_loop(0, tiles, body, 0)
            got[layer, tensor, block_of(chunk, me)] = sent[tensor, chunk, me]

    def project_decode(layer):
        dec_h[0:PAD] = rows_h[2 * blk:2 * blk + PAD]
        dec_h[head_dim:head_dim + PAD] = rows_h[2 * blk:2 * blk + PAD]
        for tensor in range(3):
            dec_copy(layer, tensor).wait()
            flat = lax.dot_general(dec_w[tensor], dec_h[...], (((1,), (1,)), ((), ())), preferred_element_type=F32)
            if tensor != 2:
                flat = rotate(flat, 2)
            if tensor == 0:
                row = lax.broadcasted_iota(jnp.int32, flat.shape, 0) // head_dim
                col = lax.broadcasted_iota(jnp.int32, flat.shape, 1) // head_dim
                dec_q[...] = jnp.where(row == col, flat, 0.0).astype(BF16)
            elif tensor == 1:
                dec_k[...] = flat.T.astype(BF16)
            else:
                dec_v[...] = flat.astype(BF16)

        @pl.when(layer < last)
        def _():
            for tensor in range(3):
                dec_copy(layer + 1, tensor).start()

    def turn_keys(layer, chunk):
        def body(i, carry):
            for u in range(4):
                j = chunk * group + 4 * i + u
                key_rows[pl.ds(pl.multiple_of(j * blk, blk), blk), :] = got[layer, 1, j].astype(F32).T.astype(BF16)
            return carry

        lax.fori_loop(0, group // 4, body, 0)

    def save_cache(layer, chunk):
        def body(i, carry):
            j = chunk * group + i
            place = pl.ds(pl.multiple_of(j * blk, blk), blk)
            pltpu.make_async_copy(got.at[layer, 1, j], k_cache.at[layer, :, place], sem_cache.at[layer, 0]).start()
            pltpu.make_async_copy(got.at[layer, 2, j], v_cache.at[layer, :, place], sem_cache.at[layer, 1]).start()
            return carry

        lax.fori_loop(0, group, body, 0)

    def scores(layer, pair, tile, slot):
        keys = key_rows[pl.ds(pl.multiple_of(tile * KEY_TILE, KEY_TILE), KEY_TILE), :]
        for u in range(2):
            query = jnp.concatenate([got[layer, 0, pair_blocks * pair + 2 * u], got[layer, 0, pair_blocks * pair + 2 * u + 1]], axis=1)
            blank = jnp.zeros((head_dim, query.shape[1]), BF16)
            for h in range(heads_dev):
                parts = [blank] * heads_dev
                parts[h] = query[h * head_dim:(h + 1) * head_dim]
                value = jnp.dot(keys, jnp.concatenate(parts, axis=0), preferred_element_type=F32)
                score[slot, 2 * u + h] = value
                best[slot, 2 * u + h] = jnp.max(value, axis=0, keepdims=True)

    def absorb(layer, tile, slot, place):
        held = [got[layer, 2, tile * pair_blocks + i] for i in range(pair_blocks)]
        ones = jnp.ones((acc_rows - head_dim, KEY_TILE), BF16)
        for u in range(2):
            for h in range(heads_dev):
                c = 2 * u + h
                old = run_max[place, c]
                new = jnp.maximum(old, best[slot, c])
                probs = jnp.exp2((score[slot, c] - new) * exp_scale).astype(BF16)
                shrink = jnp.exp2((old - new) * exp_scale)
                value = jnp.concatenate([jnp.concatenate([b[h * head_dim:(h + 1) * head_dim] for b in held], axis=1), ones], axis=0)
                run_max[place, c] = new
                run_acc[place, c] = run_acc[place, c] * shrink + jnp.dot(value, probs, preferred_element_type=F32)

    def mask_diagonal(slot):
        key = lax.broadcasted_iota(jnp.int32, score.shape[2:], 0)
        query = lax.broadcasted_iota(jnp.int32, score.shape[2:], 1)
        for u in range(2):
            for h in range(heads_dev):
                value = jnp.where(key <= query + u * score.shape[3], score[slot, 2 * u + h], -jnp.inf)
                score[slot, 2 * u + h] = value
                best[slot, 2 * u + h] = jnp.max(value, axis=0, keepdims=True)

    def fresh_state(place):
        run_max[place] = jnp.full(run_max.shape[1:], -jnp.inf, F32)
        run_acc[place] = jnp.zeros(run_acc.shape[1:], F32)

    def hand_out(layer, chunk, pair, place):
        for u in range(2):
            full = jnp.concatenate(
                [run_acc[place, 2 * u + h, :head_dim] / run_acc[place, 2 * u + h, head_dim:head_dim + 1] for h in range(heads_dev)], axis=0
            )
            turned = full.T.astype(BF16)
            for i in range(2):
                j = pair_blocks * pair + 2 * u + i
                mixed_sent[j] = turned[i * blk:(i + 1) * blk]
                device = j if chunk == 0 else blocks - 1 - j
                where = mixed.at[layer, chunk * blk:(chunk + 1) * blk, pl.ds(pl.multiple_of(me * LANES, LANES), LANES)]
                send_to(remote(mixed_sent.at[j], where, send_o.at[chunk], recv_o.at[layer, chunk], device), device)

                @pl.when(device == me)
                def _(j=j):
                    mixed[layer, chunk * blk:(chunk + 1) * blk, pl.ds(pl.multiple_of(me * LANES, LANES), LANES)] = mixed_sent[j]

    def triangle(s):
        j = sum((s >= (k * (k + 1)) // 2).astype(jnp.int32) for k in range(1, pairs))
        return j, s - (j * (j + 1)) // 2

    def attend_triangle(layer, chunk):
        base = chunk * pairs
        count = pairs * (pairs + 1) // 2

        def one(s, slot):
            pair, tile = triangle(s)
            after, after_tile = triangle(jnp.minimum(s + 1, count - 1))
            if chunk == 0:
                @pl.when(tile == 0)
                def _():
                    fresh_state(pair)

            @pl.when(tile == pair)
            def _():
                mask_diagonal(slot)

            scores(layer, base + after, base + after_tile, 1 - slot)
            absorb(layer, base + tile, slot, pair)

            @pl.when(tile == pair)
            def _():
                hand_out(layer, chunk, base + pair, pair)

        scores(layer, base, base, 0)

        def body(i, carry):
            one(2 * i, 0)
            one(2 * i + 1, 1)
            return carry

        lax.fori_loop(0, count // 2, body, 0)

    def attend_square(layer):
        count = pairs * pairs

        def one(s, slot):
            pair, tile = s // pairs, lax.rem(s, pairs)
            after = jnp.minimum(s + 1, count - 1)

            @pl.when(tile == 0)
            def _():
                fresh_state(pair)

            scores(layer, pairs + after // pairs, lax.rem(after, pairs), 1 - slot)
            absorb(layer, tile, slot, pair)

        scores(layer, pairs, 0, 0)

        def body(i, carry):
            one(2 * i, 0)
            one(2 * i + 1, 1)
            return carry

        lax.fori_loop(0, count // 2, body, 0)

    def attend_decode(layer):
        ones = jnp.ones((PAD, KEY_TILE), BF16)
        queries = dec_q[...]

        def step(value_rows, value, carry):
            old, total = carry
            new = jnp.maximum(old, jnp.max(value, axis=0, keepdims=True))
            probs = jnp.exp2((value - new) * exp_scale).astype(BF16)
            shrink = jnp.exp2((old - new) * exp_scale)
            return new, total * shrink + jnp.dot(value_rows, probs, preferred_element_type=F32)

        def body(tile, carry):
            keys = key_rows[pl.ds(pl.multiple_of(tile * KEY_TILE, KEY_TILE), KEY_TILE), :]
            value = jnp.dot(keys, queries, preferred_element_type=F32)
            held = jnp.concatenate([got[layer, 2, tile * pair_blocks + i] for i in range(pair_blocks)], axis=1)
            return step(jnp.concatenate([held, ones], axis=0), value, carry)

        state = (jnp.full((1, LANES), -jnp.inf, F32), jnp.zeros((LANES + PAD, LANES), F32))
        state = lax.fori_loop(0, blocks // pair_blocks, body, state)
        value = jnp.dot(dec_k[...], queries, preferred_element_type=F32)
        key = lax.broadcasted_iota(jnp.int32, value.shape, 0)
        query = lax.rem(lax.broadcasted_iota(jnp.int32, value.shape, 1), head_dim)
        value = jnp.where((key <= query) & (key < steps), value, -jnp.inf)
        held = jnp.concatenate([dec_v[...], ones[:, :LANES]], axis=0)
        _, total = step(held, value, state)
        turned = (total[:LANES] / total[LANES:LANES + 1]).T
        lane = lax.broadcasted_iota(jnp.int32, (PAD, LANES), 1)
        result = turned[0:PAD]
        for h in range(1, heads_dev):
            result = jnp.where(lane >= h * head_dim, turned[h * head_dim:h * head_dim + PAD], result)
        dec_sent[...] = result.astype(BF16)
        mine = pl.ds(pl.multiple_of(me * LANES, LANES), LANES)
        mixed[layer, 2 * blk:2 * blk + PAD, mine] = dec_sent[...]

        def send(i, carry):
            device = lax.rem(me + 1 + i, group)
            remote(dec_sent, mixed.at[layer, 2 * blk:2 * blk + PAD, mine], send_d, recv_d.at[layer], device).start()
            return carry

        lax.fori_loop(0, others, send, 0)

    def dense(layer, chunk, between):
        row0, count = (0, blk) if chunk == 0 else (blk, b_rows)
        rows = slice(row0, row0 + count)
        for n in range(tiles):
            if chunk == 0:
                wo_copy(layer, n).wait()
            cols = slice(n * QKV_ROWS, (n + 1) * QKV_ROWS)
            added = rows_x[rows, cols].astype(F32) + jnp.dot(mixed[layer, rows, :], wo_buf[n], preferred_element_type=F32)
            acc[:count, cols] = added.astype(BF16).astype(F32)
        if chunk == 1:
            @pl.when(layer < last)
            def _():
                for n in range(tiles):
                    wo_copy(layer + 1, n).start()

        normalize(lambda r: acc[r, :], row0, count, gain_mlp[layer])

        def step_at(k):
            return k if chunk == 0 else ff_steps - 1 - k

        def widen(k):
            step = step_at(k)
            slot = lax.rem(step, FF_SLOTS)

            def ready():
                for copy in gu_copies(layer, step):
                    copy.wait()

            if chunk == 0:
                ready()
            else:
                pl.when(k >= FF_SLOTS)(ready)
            normed = rows_h[rows, :]
            gate = jnp.dot(normed, gate_ring[slot], preferred_element_type=F32)
            upward = jnp.dot(normed, up_ring[slot], preferred_element_type=F32)
            gated[:count] = (jax.nn.silu(gate) * upward).astype(BF16)

        def narrow(k):
            step = step_at(k)
            slot = lax.rem(step, FF_SLOTS)

            def ready():
                down_copy(layer, step).wait()

            if chunk == 0:
                ready()
            else:
                pl.when(k >= FF_SLOTS)(ready)
            acc[:count] += jnp.dot(gated[:count], down_ring[slot], preferred_element_type=F32)

        def refill(k, start):
            if chunk == 0:
                @pl.when(k + FF_SLOTS < ff_steps)
                def _():
                    start(layer, k + FF_SLOTS)
            else:
                step = step_at(k)

                @pl.when(step >= FF_SLOTS)
                def _():
                    start(layer, step - FF_SLOTS)

                @pl.when((step < FF_SLOTS) & (layer < last))
                def _():
                    start(layer + 1, step)

        def start_gu(which, step):
            for copy in gu_copies(which, step):
                copy.start()

        def start_down(which, step):
            down_copy(which, step).start()

        widen(0)
        refill(0, start_gu)

        def body(k, carry):
            narrow(k - 1)
            widen(k)
            refill(k - 1, start_down)
            refill(k, start_gu)
            return carry

        if between is None:
            lax.fori_loop(1, ff_steps, body, 0)
        else:
            lax.fori_loop(1, SPLIT, body, 0)
            between()
            lax.fori_loop(SPLIT, ff_steps, body, 0)
        narrow(ff_steps - 1)
        refill(ff_steps - 1, start_down)
        rows_x[rows, :] = acc[:count].astype(BF16)

    pltpu.make_async_copy(x_in, rows_x.at[0:2 * blk], sem_x).start()
    for r in range(tiles):
        qkv_copy(0, order_a[0], r).start()
    for tensor in range(3):
        dec_copy(0, tensor).start()
    for n in range(tiles):
        wo_copy(0, n).start()
    for step in range(FF_SLOTS):
        for copy in gu_copies(0, step):
            copy.start()
        down_copy(0, step).start()

    barrier = pltpu.get_barrier_semaphore()
    for i in range(1, group):
        pl.semaphore_signal(barrier, inc=1, device_id={"cp": lax.rem(me + i, group)}, device_id_type=MESH)
    dec_h[...] = jnp.zeros_like(dec_h)
    pltpu.make_async_copy(x_in, rows_x.at[0:2 * blk], sem_x).wait()
    normalize_x(0, 2 * blk, gain_attn[0])
    pl.semaphore_wait(barrier, others)

    my_cols = pl.ds(pl.multiple_of(me * LANES, LANES), LANES)

    def part_out(i, carry):
        device = lax.rem(me + 1 + i, group)
        cols = pl.ds(pl.multiple_of(device * LANES, LANES), LANES)
        remote(emb_in.at[:, cols], emb_part.at[me], send_e, recv_e, device).start()
        return carry

    lax.fori_loop(0, others, part_out, 0)
    emb_part[me] = emb_in[:, my_cols]
    project(0, 0)
    wait_recv(emb_part.at[0:others], recv_e)
    emb_sum[...] = jnp.sum(emb_part[...].astype(F32), axis=0).astype(BF16)
    emb_full[:, my_cols] = emb_sum[...]

    def sum_out(i, carry):
        device = lax.rem(me + 1 + i, group)
        remote(emb_sum, emb_full.at[:, my_cols], send_f, recv_f, device).start()
        return carry

    lax.fori_loop(0, others, sum_out, 0)

    def layer_body(layer, carry):
        project(layer, 1)

        @pl.when(layer == 0)
        def _():
            wait_recv(emb_part.at[0:others], recv_f)
            rows_x[2 * blk:2 * blk + PAD] = emb_full[...]
            wide = emb_full[...].astype(F32)
            inv = lax.rsqrt(jnp.mean(wide * wide, axis=-1, keepdims=True) + NORM_EPS)
            rows_h[2 * blk:2 * blk + PAD] = (wide * inv * gain_attn[0]).astype(BF16)

        project_decode(layer)
        for tensor in range(3):
            wait_recv(got.at[layer, tensor, 0:others], recv_qkv.at[layer, 0, tensor])
        turn_keys(layer, 0)
        save_cache(layer, 0)
        attend_triangle(layer, 0)
        send_all(layer, 1, 1)
        send_all(layer, 2, 1)
        wait_recv(got.at[layer, 0, 0:others], recv_qkv.at[layer, 1, 0])
        attend_square(layer)
        for tensor in range(3):
            wait_send(sent.at[tensor, 0, 0:others], send_qkv.at[0, tensor])
        wait_recv(mixed_sent.at[0:others], recv_o.at[layer, 0])

        def finish_attention():
            for tensor in (1, 2):
                wait_recv(got.at[layer, tensor, 0:others], recv_qkv.at[layer, 1, tensor])
            turn_keys(layer, 1)
            attend_triangle(layer, 1)
            attend_decode(layer)
            save_cache(layer, 1)

        dense(layer, 0, finish_attention)
        for tensor in range(3):
            wait_send(sent.at[tensor, 1, 0:others], send_qkv.at[1, tensor])
        wait_send(mixed_sent.at[0:others], send_o.at[0])

        @pl.when(layer < last)
        def _():
            normalize_x(0, blk, gain_attn[layer + 1])
            project(layer + 1, 0)

        @pl.when(layer == last)
        def _():
            pltpu.make_async_copy(rows_x.at[0:blk], x_out.at[0:blk], sem_out.at[0]).start()

        wait_recv(mixed_sent.at[0:others], recv_o.at[layer, 1])
        wait_recv(emb_part.at[0:others], recv_d.at[layer])
        dense(layer, 1, None)
        wait_send(mixed_sent.at[0:others], send_o.at[1])
        wait_send(emb_part.at[0:others], send_d)

        @pl.when(layer < last)
        def _():
            normalize_x(blk, b_rows, gain_attn[layer + 1])

        return carry

    lax.fori_loop(0, num_layers, layer_body, 0)

    pltpu.make_async_copy(rows_x.at[blk:2 * blk], x_out.at[blk:2 * blk], sem_out.at[1]).start()
    dec_out[...] = rows_x[2 * blk:2 * blk + PAD]
    wait_send(emb_part.at[0:others], send_e)
    wait_send(emb_part.at[0:others], send_f)
    for layer in range(num_layers):
        pltpu.make_async_copy(k_cache.at[layer], k_cache.at[layer], sem_cache.at[layer, 0]).wait()
        pltpu.make_async_copy(v_cache.at[layer], v_cache.at[layer], sem_cache.at[layer, 1]).wait()
    for part in range(2):
        where = pl.ds(part * blk, blk)
        pltpu.make_async_copy(rows_x.at[where], x_out.at[where], sem_out.at[part]).wait()


def solution(mesh):
    group = mesh.shape["cp"]

    def local_program(x_rows, token_ids, table_rows, norm_attn, w_q, w_k, w_v, w_o, norm_mlp, w_gate, w_up, w_down):
        device = lax.axis_index("cp")
        num_layers, d_model, num_heads, head_dim = w_q.shape
        kv_heads = w_k.shape[2]
        ff_dim = w_gate.shape[2]
        seq_dev = x_rows.shape[0]
        blk = seq_dev // 2
        seq_len = group * seq_dev
        steps = token_ids.shape[0]
        heads_dev = num_heads // group
        assert heads_dev * head_dim == LANES and kv_heads == num_heads and blk == LANES

        emb = pick_rows(token_ids, (device * table_rows.shape[0]).reshape(1), table_rows)

        offsets = jnp.arange(LANES, dtype=jnp.int32)
        positions = jnp.stack([device * blk + offsets, (2 * group - 1 - device) * blk + offsets, seq_len + offsets % head_dim])
        inv_freq = 1.0 / (ROPE_BASE ** (jnp.arange(0, head_dim, 2, dtype=F32) / head_dim))
        angles = positions.astype(F32)[:, None, :] * inv_freq[None, :, None]
        tables = jnp.stack([jnp.cos(angles), jnp.sin(angles)], axis=1).reshape(6, head_dim // 2, LANES)

        def head_rows(w):
            return w.transpose(0, 2, 3, 1).reshape(num_layers * num_heads * head_dim, d_model)

        any_spec = pl.BlockSpec(memory_space=pl.ANY)
        vmem = pl.BlockSpec(memory_space=pltpu.VMEM)
        dma = pltpu.SemaphoreType.DMA
        acc_rows = head_dim + 8
        quarter = KEY_TILE // 2
        tiles = d_model // QKV_ROWS
        pairs = group * blk // KEY_TILE
        scratch = [
            pltpu.VMEM((2 * blk + PAD, d_model), BF16),
            pltpu.VMEM((2 * blk + PAD, d_model), BF16),
            pltpu.VMEM((num_layers, 2 * blk + PAD, d_model), BF16),
            pltpu.VMEM((3, 2, group, LANES, blk), BF16),
            pltpu.VMEM((num_layers, 3, 2 * group, LANES, blk), BF16),
            pltpu.VMEM((seq_len, LANES), BF16),
            pltpu.VMEM((2 * group, blk, LANES), BF16),
            pltpu.VMEM((2, 2 * heads_dev, KEY_TILE, quarter), F32),
            pltpu.VMEM((2, 2 * heads_dev, 1, quarter), F32),
            pltpu.VMEM((pairs, 2 * heads_dev, 1, quarter), F32),
            pltpu.VMEM((pairs, 2 * heads_dev, acc_rows, quarter), F32),
            pltpu.VMEM((tiles, QKV_ROWS, d_model), BF16),
            pltpu.VMEM((tiles, d_model, QKV_ROWS), BF16),
            pltpu.VMEM((FF_SLOTS, d_model, FF_TILE), BF16),
            pltpu.VMEM((FF_SLOTS, d_model, FF_TILE), BF16),
            pltpu.VMEM((FF_SLOTS, FF_TILE, d_model), BF16),
            pltpu.VMEM((3, LANES, d_model), BF16),
            pltpu.VMEM((LANES, d_model), BF16),
            pltpu.VMEM((LANES, LANES), BF16),
            pltpu.VMEM((LANES, LANES), BF16),
            pltpu.VMEM((LANES, LANES), BF16),
            pltpu.VMEM((blk + PAD, d_model), F32),
            pltpu.VMEM((blk + PAD, FF_TILE), BF16),
            pltpu.VMEM((group, PAD, LANES), BF16),
            pltpu.VMEM((PAD, d_model), BF16),
            pltpu.VMEM((PAD, LANES), BF16),
            pltpu.VMEM((PAD, LANES), BF16),
            dma, dma((tiles,)), dma((tiles,)), dma((3, FF_SLOTS)), dma((3,)),
            dma((2, 3)), dma((num_layers, 2, 3)), dma((2,)), dma((num_layers, 2)), dma, dma((num_layers,)),
            dma, dma, dma, dma, dma((num_layers, 2)), dma((2,)),
        ]
        x_new, k_flat, v_flat, dec = pl.pallas_call(
            functools.partial(main_kernel, group, head_dim, num_layers, steps),
            out_shape=(
                jax.ShapeDtypeStruct((seq_dev, d_model), BF16),
                jax.ShapeDtypeStruct((num_layers, LANES, seq_len), BF16),
                jax.ShapeDtypeStruct((num_layers, LANES, seq_len), BF16),
                jax.ShapeDtypeStruct((PAD, d_model), BF16),
            ),
            in_specs=[any_spec, vmem, vmem, vmem, vmem] + [any_spec] * 7,
            out_specs=(any_spec, any_spec, any_spec, vmem),
            scratch_shapes=scratch,
            compiler_params=pltpu.CompilerParams(collective_id=0, has_side_effects=True, vmem_limit_bytes=66_000_000),
            name="prefill_decode",
        )(
            x_rows, emb, norm_attn.astype(F32)[:, None, :], norm_mlp.astype(F32)[:, None, :], tables,
            head_rows(w_q), head_rows(w_k), head_rows(w_v), w_o.reshape(num_layers * d_model, d_model),
            w_gate.reshape(num_layers * d_model, ff_dim), w_up.reshape(num_layers * d_model, ff_dim), w_down.reshape(num_layers * ff_dim, d_model),
        )

        def cache(flat):
            return flat.reshape(num_layers, heads_dev, head_dim, seq_len).transpose(0, 3, 1, 2)

        return x_new, cache(k_flat), cache(v_flat), dec[:steps]

    replicated = P()
    in_specs = (P(("req", "cp"), None), P("req"), P("cp", None)) + (replicated,) * 9
    out_specs = (P(("req", "cp"), None), P(None, "req", "cp", None), P(None, "req", "cp", None), P("req", None))
    return jax.shard_map(local_program, mesh=mesh, in_specs=in_specs, out_specs=out_specs, check_vma=False)
```

time: 1280 us -> 290 us (0.23); the launches traced: 1260 us -> 291 us
  local copies, waits for them, and re-layouts: 411 us -> 12.6 us
  matrix products: 373 us -> 0 us
  Pallas kernels: 0 us -> 277 us
  blocking collectives: 230 us -> 0 us
  waiting for transfers between devices: 109 us -> 0 us
  other arithmetic: 106 us -> 0.94 us
  starting transfers between devices: 15.5 us -> 0 us
  between operations: 15 us -> 0.68 us
    dot_general x26 -> x0, matrix products: 347 us -> none  [the longest x4 107 us: attend(): jnp.einsum('qhgd,khd->hgqk', grouped, keys, preferred_element_type=jnp.fl...]
    pallas_call x0 -> x2, Pallas kernels: none -> 277 us  [the longest x1 275 us: local_program(): pl.pallas_call(functools.partial(main_kernel, group, head_dim, num_layers...]
    psum x5 -> x0, blocking collectives: 230 us -> none  [the longest x4 183 us: local_program(): lax.psum(partial, 'cp')]
    unnamed x95 -> x3, local copies, waits for them, and re-layouts: 193 us -> 8.56 us
    slice x13 -> x1, local copies, waits for them, and re-layouts: 184 us -> 1.37 us  [local_program(): return (x_new, cache(k_flat), cache(v_flat), dec[:steps])]
    all_gather x4 -> x0, waiting for transfers between devices: 87.9 us -> none  [the longest x2 83.4 us: local_program(): all_keys = lax.all_gather(keys, 'cp', axis=0, tiled=True)]
    reduce_sum x9 -> x0, other arithmetic: 83.5 us -> none  [the longest x4 82.6 us: attend(): attn_probs = jax.nn.softmax(scores, axis=-1).astype(jnp.bfloat16)]
    unnamed x6 -> x0, matrix products: 26.1 us -> none
  transfers between devices with their start and end apart: 6 -> 0, of which waited for: 3 -> 0; matrix products, arithmetic and copies ran while one was open for 50% -> 0% of each run, Pallas kernels for 0% -> 0%
where the time goes in v1:
time: 290 us; the launch traced here: 291 us
  Pallas kernels  277 us (96%)
  local copies, waits for them, and re-layouts  12.6 us (4%)
    pallas_call x1, Pallas kernels, local_program(): pl.pallas_call(functools.partial(main_kernel, group, head_dim, num_layers...  275 us
    unnamed x3, local copies, waits for them, and re-layouts  8.56 us

profile of v1, /device:TPU:23, one launch (start us, length us, event | category | flops | bytes accessed | tf_op | source)
XLA Modules:
  0.0 291.1 jit_solution(15474963208041116055)
XLA Ops:
  0.7 1.3 reshape.125.gain_attn
  2.0 1.3 reshape.126.gain_mlp
  3.3 2.3 pick_rows.1.emb_in
  5.6 0.3 multiply_cosine_fusion
  5.9 0.7 pad_maximum_fusion
  6.5 274.6 %prefill_decode.1 = (bf16[256,2048]{1,0:T(8,128)(2,1)}, bf16[2,128,4096]{2,1,0:T(8,128)(2,1)}, bf16[2,128,4096]{2,1,0:T(8,128)(2,1)}, bf16[16,2048]{1,0:T(8,128)(2,1)}) custom-call(bf16[256,2048]{1,0:T(8,128)(2,1)} %x_in.1, bf16[16,2048]{1,0:T(8,128)(2,1)} %pick_rows.1.emb_in, f32[2,1,2048]{2,1,0:T(1,128)} %reshape.125.gain_attn, ...), custom_call_target="tpu_custom_call" | custom-call | tf_op jit(solution)/shard_map/prefill_decode/pallas_call | solution.py:677
  281.2 1.4 slice.3
  282.5 2.3 copy.19
  284.8 3.1 %copy.20 = bf16[2,4096,2,64]{1,3,2,0:T(8,128)(2,1)} copy(bf16[2,4096,2,64]{1,3,2,0:T(8,128)(2,1)} %bitcast.26) | data formatting | bytes 4194304
  288.0 3.1 %copy.21 = bf16[2,4096,2,64]{1,3,2,0:T(8,128)(2,1)} copy(bf16[2,4096,2,64]{1,3,2,0:T(8,128)(2,1)} %bitcast.25) | data formatting | bytes 4194304
  (4 shorter events, 0.0 us)

commit v2 on v1

--- a/solution.py
+++ b/solution.py
@@ -17,9 +17,9 @@
 PAD = 16
 QKV_ROWS = 512
 FF_TILE = 512
-FF_SLOTS = 3
+FF_SLOTS = 4
 KEY_TILE = 512
-SPLIT = 11
+SPLIT = (14, 12)
 
 
 def pick_kernel(vocab_dev, ids_ref, base_ref, table_ref, out_ref, rows, sems):
@@ -67,7 +67,7 @@
     group, head_dim, num_layers, steps,
     x_in, emb_in, gain_attn, gain_mlp, tables, w_q, w_k, w_v, w_o, w_gate, w_up, w_down,
     x_out, k_cache, v_cache, dec_out,
-    rows_x, rows_h, mixed, sent, got, key_rows, mixed_sent, score, best, run_max, run_acc,
+    rows_x, rows_h, mixed, sent, got_q, got, key_rows, mixed_sent, score, best, run_max, run_acc,
     qkv_ring, wo_buf, gate_ring, up_ring, down_ring, dec_w, dec_h, dec_q, dec_k, dec_v, acc, gated, emb_part, emb_full, emb_sum, dec_sent,
     sem_x, sem_qkv, sem_wo, sem_ff, sem_dec, send_qkv, recv_qkv, send_o, recv_o, send_d, recv_d, send_e, recv_e, send_f, recv_f, sem_cache, sem_out,
 ):
@@ -133,9 +133,12 @@
     def block_of(chunk, device):
         return device if chunk == 0 else blocks - 1 - device
 
+    def home(layer, tensor):
+        return got_q if tensor == 0 else got.at[layer, tensor - 1]
+
     def qkv_piece(layer, tensor, chunk, device):
         return remote(
-            sent.at[tensor, chunk, device], got.at[layer, tensor, block_of(chunk, me)],
+            sent.at[tensor, chunk, device], home(layer, tensor).at[block_of(chunk, me)],
             send_qkv.at[chunk, tensor], recv_qkv.at[layer, chunk, tensor], device,
         )
 
@@ -144,13 +147,28 @@
         def _():
             piece.start()
 
-    def send_all(layer, tensor, chunk):
+    def send_queries(layer):
+        def body(i, carry):
+            qkv_piece(layer, 0, 1, lax.rem(me + 1 + i, group)).start()
+            return carry
+
+        lax.fori_loop(0, others, body, 0)
+
+    def send_rest(layer):
         def body(i, carry):
             device = lax.rem(me + 1 + i, group)
-            qkv_piece(layer, tensor, chunk, device).start()
+            source, place = sent.at[pl.ds(1, 2), 1, device], got.at[layer, pl.ds(0, 2), block_of(1, me)]
+            remote(source, place, send_qkv.at[1, 1], recv_qkv.at[layer, 1, 1], device).start()
             return carry
 
         lax.fori_loop(0, others, body, 0)
+
+    def gain_of(ref, layer):
+        gains = ref[...].astype(F32)
+        chosen = gains[0:1]
+        for n in range(1, num_layers):
+            chosen = jnp.where(layer == n, gains[n:n + 1], chosen)
+        return chosen
 
     def normalize(read, row0, count, gain):
         part = 64 if count % 64 == 0 else 48
@@ -177,32 +195,40 @@
         turned = jnp.concatenate([first * cosines - second * sines, second * cosines + first * sines], axis=1)
         return turned.reshape(flat.shape)
 
-    def project(layer, chunk):
+    def project(layer, chunk, after_first=None):
         order = order_a if chunk == 0 else order_a[::-1]
         for place, tensor in enumerate(order):
-            def body(r, carry, place=place, tensor=tensor):
+            def body(i, carry, place=place, tensor=tensor):
+                spots = (2 * i, 2 * i + 1)
                 if chunk == 0 or place > 0:
-                    qkv_copy(layer, tensor, r).wait()
-                flat = lax.dot_general(
-                    qkv_ring[r], rows_h[chunk * blk:(chunk + 1) * blk, :], (((1,), (1,)), ((), ())), preferred_element_type=F32
-                )
-                if tensor != 2:
-                    flat = rotate(flat, chunk)
-                first = tile_of(r) * per_tile
-                sent[tensor, chunk, pl.ds(first, per_tile)] = flat.astype(BF16).reshape(per_tile, LANES, blk)
-                if chunk == 0 or tensor == 0:
-                    for i in range(per_tile):
-                        send_to(qkv_piece(layer, tensor, chunk, first + i), first + i)
-                if place < 2:
-                    qkv_copy(layer, order[place + 1], r).start()
-                elif chunk == 1:
-                    @pl.when(layer < last)
-                    def _():
-                        qkv_copy(layer + 1, order_a[0], r).start()
+                    for r in spots:
+                        qkv_copy(layer, tensor, r).wait()
+                for r in spots:
+                    flat = lax.dot_general(
+                        qkv_ring[r], rows_h[chunk * blk:(chunk + 1) * blk, :], (((1,), (1,)), ((), ())), preferred_element_type=F32
+                    )
+                    if tensor != 2:
+                        flat = rotate(flat, chunk)
+                    sent[tensor, chunk, pl.ds(tile_of(r) * per_tile, per_tile)] = flat.astype(BF16).reshape(per_tile, LANES, blk)
+                for r in spots:
+                    if place < 2:
+                        qkv_copy(layer, order[place + 1], r).start()
+                    elif chunk == 1:
+                        @pl.when(layer < last)
+                        def _(r=r):
+                            qkv_copy(layer + 1, order_a[0], r).start()
+                    if chunk == 0:
+                        for k in range(per_tile):
+                            device = tile_of(r) * per_tile + k
+                            send_to(qkv_piece(layer, tensor, chunk, device), device)
                 return carry
 
-            lax.fori_loop(0, tiles, body, 0)
-            got[layer, tensor, block_of(chunk, me)] = sent[tensor, chunk, me]
+            lax.fori_loop(0, tiles // 2, body, 0)
+            home(layer, tensor)[block_of(chunk, me)] = sent[tensor, chunk, me]
+            if chunk == 1 and tensor == 0:
+                send_queries(layer)
+            if place == 0 and after_first is not None:
+                after_first()
 
     def project_decode(layer):
         dec_h[0:PAD] = rows_h[2 * blk:2 * blk + PAD]
@@ -230,7 +256,7 @@
         def body(i, carry):
             for u in range(4):
                 j = chunk * group + 4 * i + u
-                key_rows[pl.ds(pl.multiple_of(j * blk, blk), blk), :] = got[layer, 1, j].astype(F32).T.astype(BF16)
+                key_rows[pl.ds(pl.multiple_of(j * blk, blk), blk), :] = got[layer, 0, j].astype(F32).T.astype(BF16)
             return carry
 
         lax.fori_loop(0, group // 4, body, 0)
@@ -239,8 +265,8 @@
         def body(i, carry):
             j = chunk * group + i
             place = pl.ds(pl.multiple_of(j * blk, blk), blk)
-            pltpu.make_async_copy(got.at[layer, 1, j], k_cache.at[layer, :, place], sem_cache.at[layer, 0]).start()
-            pltpu.make_async_copy(got.at[layer, 2, j], v_cache.at[layer, :, place], sem_cache.at[layer, 1]).start()
+            pltpu.make_async_copy(got.at[layer, 0, j], k_cache.at[layer, :, place], sem_cache.at[layer, 0]).start()
+            pltpu.make_async_copy(got.at[layer, 1, j], v_cache.at[layer, :, place], sem_cache.at[layer, 1]).start()
             return carry
 
         lax.fori_loop(0, group, body, 0)
@@ -248,7 +274,7 @@
     def scores(layer, pair, tile, slot):
         keys = key_rows[pl.ds(pl.multiple_of(tile * KEY_TILE, KEY_TILE), KEY_TILE), :]
         for u in range(2):
-            query = jnp.concatenate([got[layer, 0, pair_blocks * pair + 2 * u], got[layer, 0, pair_blocks * pair + 2 * u + 1]], axis=1)
+            query = jnp.concatenate([got_q[pair_blocks * pair + 2 * u], got_q[pair_blocks * pair + 2 * u + 1]], axis=1)
             blank = jnp.zeros((head_dim, query.shape[1]), BF16)
             for h in range(heads_dev):
                 parts = [blank] * heads_dev
@@ -257,134 +283,126 @@
                 score[slot, 2 * u + h] = value
                 best[slot, 2 * u + h] = jnp.max(value, axis=0, keepdims=True)
 
-    def absorb(layer, tile, slot, place):
-        held = [got[layer, 2, tile * pair_blocks + i] for i in range(pair_blocks)]
-        ones = jnp.ones((acc_rows - head_dim, KEY_TILE), BF16)
+    def absorb(layer, tile, slot, place, diagonal=False, first=False):
+        held = [got[layer, 1, tile * pair_blocks + i] for i in range(pair_blocks)]
         for u in range(2):
+            count = pair_blocks // 2 if diagonal and u == 0 else pair_blocks
+            ones = jnp.ones((acc_rows - head_dim, count * blk), BF16)
             for h in range(heads_dev):
                 c = 2 * u + h
-                old = run_max[place, c]
-                new = jnp.maximum(old, best[slot, c])
-                probs = jnp.exp2((score[slot, c] - new) * exp_scale).astype(BF16)
-                shrink = jnp.exp2((old - new) * exp_scale)
-                value = jnp.concatenate([jnp.concatenate([b[h * head_dim:(h + 1) * head_dim] for b in held], axis=1), ones], axis=0)
+                new = best[slot, c] if first else jnp.maximum(run_max[place, c], best[slot, c])
+                probs = jnp.exp2((score[slot, c, :count * blk] - new) * exp_scale).astype(BF16)
+                value = jnp.concatenate([jnp.concatenate([b[h * head_dim:(h + 1) * head_dim] for b in held[:count]], axis=1), ones], axis=0)
+                added = jnp.dot(value, probs, preferred_element_type=F32)
+                if first:
+                    run_acc[place, c] = added
+                else:
+                    run_acc[place, c] = run_acc[place, c] * jnp.exp2((run_max[place, c] - new) * exp_scale) + added
                 run_max[place, c] = new
-                run_acc[place, c] = run_acc[place, c] * shrink + jnp.dot(value, probs, preferred_element_type=F32)
 
     def mask_diagonal(slot):
-        key = lax.broadcasted_iota(jnp.int32, score.shape[2:], 0)
-        query = lax.broadcasted_iota(jnp.int32, score.shape[2:], 1)
+        width = score.shape[3]
+        key = lax.broadcasted_iota(jnp.int32, (width, width), 0)
+        query = lax.broadcasted_iota(jnp.int32, (width, width), 1)
         for u in range(2):
+            rows = slice(u * width, (u + 1) * width)
             for h in range(heads_dev):
-                value = jnp.where(key <= query + u * score.shape[3], score[slot, 2 * u + h], -jnp.inf)
-                score[slot, 2 * u + h] = value
-                best[slot, 2 * u + h] = jnp.max(value, axis=0, keepdims=True)
-
-    def fresh_state(place):
-        run_max[place] = jnp.full(run_max.shape[1:], -jnp.inf, F32)
-        run_acc[place] = jnp.zeros(run_acc.shape[1:], F32)
-
-    def hand_out(layer, chunk, pair, place):
+                c = 2 * u + h
+                value = jnp.where(key <= query, score[slot, c, rows], -jnp.inf)
+                score[slot, c, rows] = value
+                top = jnp.max(value, axis=0, keepdims=True)
+                if u == 1:
+                    top = jnp.maximum(top, jnp.max(score[slot, c, :width], axis=0, keepdims=True))
+                best[slot, c] = top
+
+    def turn_out(place):
         for u in range(2):
             full = jnp.concatenate(
                 [run_acc[place, 2 * u + h, :head_dim] / run_acc[place, 2 * u + h, head_dim:head_dim + 1] for h in range(heads_dev)], axis=0
             )
             turned = full.T.astype(BF16)
             for i in range(2):
-                j = pair_blocks * pair + 2 * u + i
-                mixed_sent[j] = turned[i * blk:(i + 1) * blk]
-                device = j if chunk == 0 else blocks - 1 - j
-                where = mixed.at[layer, chunk * blk:(chunk + 1) * blk, pl.ds(pl.multiple_of(me * LANES, LANES), LANES)]
-                send_to(remote(mixed_sent.at[j], where, send_o.at[chunk], recv_o.at[layer, chunk], device), device)
-
-                @pl.when(device == me)
-                def _(j=j):
-                    mixed[layer, chunk * blk:(chunk + 1) * blk, pl.ds(pl.multiple_of(me * LANES, LANES), LANES)] = mixed_sent[j]
-
-    def triangle(s):
-        j = sum((s >= (k * (k + 1)) // 2).astype(jnp.int32) for k in range(1, pairs))
-        return j, s - (j * (j + 1)) // 2
+                mixed_sent[pair_blocks * place + 2 * u + i] = turned[i * blk:(i + 1) * blk]
+
+    def hand_out(layer, chunk, place):
+        mine = pl.ds(pl.multiple_of(me * LANES, LANES), LANES)
+        for i in range(pair_blocks):
+            j = pair_blocks * place + i
+            device = j if chunk == 0 else group - 1 - j
+            where = mixed.at[chunk * blk:(chunk + 1) * blk, mine]
+            send_to(remote(mixed_sent.at[j], where, send_o.at[chunk], recv_o.at[layer, chunk], device), device)
+
+            @pl.when(device == me)
+            def _(j=j):
+                mixed[chunk * blk:(chunk + 1) * blk, mine] = mixed_sent[j]
 
     def attend_triangle(layer, chunk):
         base = chunk * pairs
-        count = pairs * (pairs + 1) // 2
-
-        def one(s, slot):
-            pair, tile = triangle(s)
-            after, after_tile = triangle(jnp.minimum(s + 1, count - 1))
-            if chunk == 0:
-                @pl.when(tile == 0)
-                def _():
-                    fresh_state(pair)
-
-            @pl.when(tile == pair)
-            def _():
-                mask_diagonal(slot)
-
-            scores(layer, base + after, base + after_tile, 1 - slot)
-            absorb(layer, base + tile, slot, pair)
-
-            @pl.when(tile == pair)
-            def _():
-                hand_out(layer, chunk, base + pair, pair)
-
-        scores(layer, base, base, 0)
+        turn = me // (group // pairs)
+        first_slot = [0]
+        for pair in range(pairs - 1):
+            first_slot.append((first_slot[-1] + pair + 1) % 2)
+
+        def one_pair(pair):
+            slot = first_slot[pair]
+            for tile in range(pair + 1):
+                after = (pair, tile + 1) if tile < pair else ((pair + 1) % pairs, 0)
+                scores(layer, base + after[0], base + after[1], 1 - slot)
+                if tile == pair:
+                    mask_diagonal(slot)
+                absorb(layer, base + tile, slot, pair, diagonal=tile == pair, first=tile == 0 and chunk == 0)
+                slot = 1 - slot
+            turn_out(pair)
+            hand_out(layer, chunk, pair)
+
+        for pair in range(pairs):
+            @pl.when(turn == pair)
+            def _(pair=pair):
+                scores(layer, base + pair, base, first_slot[pair])
 
         def body(i, carry):
-            one(2 * i, 0)
-            one(2 * i + 1, 1)
-            return carry
-
-        lax.fori_loop(0, count // 2, body, 0)
+            for pair in range(pairs):
+                @pl.when(lax.rem(turn + i, pairs) == pair)
+                def _(pair=pair):
+                    one_pair(pair)
+            return carry
+
+        lax.fori_loop(0, pairs, body, 0)
 
     def attend_square(layer):
-        count = pairs * pairs
-
-        def one(s, slot):
-            pair, tile = s // pairs, lax.rem(s, pairs)
-            after = jnp.minimum(s + 1, count - 1)
-
-            @pl.when(tile == 0)
-            def _():
-                fresh_state(pair)
-
-            scores(layer, pairs + after // pairs, lax.rem(after, pairs), 1 - slot)
-            absorb(layer, tile, slot, pair)
-
         scores(layer, pairs, 0, 0)
 
-        def body(i, carry):
-            one(2 * i, 0)
-            one(2 * i + 1, 1)
-            return carry
-
-        lax.fori_loop(0, count // 2, body, 0)
+        def body(pair, carry):
+            for tile in range(pairs):
+                if tile + 1 < pairs:
+                    scores(layer, pairs + pair, tile + 1, (tile + 1) % 2)
+                else:
+                    scores(layer, pairs + jnp.minimum(pair + 1, pairs - 1), 0, 0)
+                absorb(layer, tile, tile % 2, pair, first=tile == 0)
+            return carry
+
+        lax.fori_loop(0, pairs, body, 0)
 
     def attend_decode(layer):
         ones = jnp.ones((PAD, KEY_TILE), BF16)
         queries = dec_q[...]
-
-        def step(value_rows, value, carry):
-            old, total = carry
-            new = jnp.maximum(old, jnp.max(value, axis=0, keepdims=True))
-            probs = jnp.exp2((value - new) * exp_scale).astype(BF16)
-            shrink = jnp.exp2((old - new) * exp_scale)
-            return new, total * shrink + jnp.dot(value_rows, probs, preferred_element_type=F32)
-
-        def body(tile, carry):
-            keys = key_rows[pl.ds(pl.multiple_of(tile * KEY_TILE, KEY_TILE), KEY_TILE), :]
-            value = jnp.dot(keys, queries, preferred_element_type=F32)
-            held = jnp.concatenate([got[layer, 2, tile * pair_blocks + i] for i in range(pair_blocks)], axis=1)
-            return step(jnp.concatenate([held, ones], axis=0), value, carry)
-
-        state = (jnp.full((1, LANES), -jnp.inf, F32), jnp.zeros((LANES + PAD, LANES), F32))
-        state = lax.fori_loop(0, blocks // pair_blocks, body, state)
+        wide = slice(0, LANES)
+        spots = [(i // score.shape[1], i % score.shape[1]) for i in range(blocks // pair_blocks)]
         value = jnp.dot(dec_k[...], queries, preferred_element_type=F32)
         key = lax.broadcasted_iota(jnp.int32, value.shape, 0)
         query = lax.rem(lax.broadcasted_iota(jnp.int32, value.shape, 1), head_dim)
         value = jnp.where((key <= query) & (key < steps), value, -jnp.inf)
+        top = jnp.max(value, axis=0, keepdims=True)
+        for tile, (i, j) in enumerate(spots):
+            old = jnp.dot(key_rows[tile * KEY_TILE:(tile + 1) * KEY_TILE, :], queries, preferred_element_type=F32)
+            score[i, j, :, wide] = old
+            top = jnp.maximum(top, jnp.max(old, axis=0, keepdims=True))
         held = jnp.concatenate([dec_v[...], ones[:, :LANES]], axis=0)
-        _, total = step(held, value, state)
+        total = jnp.dot(held, jnp.exp2((value - top) * exp_scale).astype(BF16), preferred_element_type=F32)
+        for tile, (i, j) in enumerate(spots):
+            held = jnp.concatenate([got[layer, 1, tile * pair_blocks + k] for k in range(pair_blocks)], axis=1)
+            probs = jnp.exp2((score[i, j, :, wide] - top) * exp_scale).astype(BF16)
+            total = total + jnp.dot(jnp.concatenate([held, ones], axis=0), probs, preferred_element_type=F32)
         turned = (total[:LANES] / total[LANES:LANES + 1]).T
         lane = lax.broadcasted_iota(jnp.int32, (PAD, LANES), 1)
         result = turned[0:PAD]
@@ -392,11 +410,11 @@
             result = jnp.where(lane >= h * head_dim, turned[h * head_dim:h * head_dim + PAD], result)
         dec_sent[...] = result.astype(BF16)
         mine = pl.ds(pl.multiple_of(me * LANES, LANES), LANES)
-        mixed[layer, 2 * blk:2 * blk + PAD, mine] = dec_sent[...]
+        mixed[2 * blk:2 * blk + PAD, mine] = dec_sent[...]
 
         def send(i, carry):
             device = lax.rem(me + 1 + i, group)
-            remote(dec_sent, mixed.at[layer, 2 * blk:2 * blk + PAD, mine], send_d, recv_d.at[layer], device).start()
+            remote(dec_sent, mixed.at[2 * blk:2 * blk + PAD, mine], send_d, recv_d.at[layer], device).start()
             return carry
 
         lax.fori_loop(0, others, send, 0)
@@ -408,15 +426,9 @@
             if chunk == 0:
                 wo_copy(layer, n).wait()
             cols = slice(n * QKV_ROWS, (n + 1) * QKV_ROWS)
-            added = rows_x[rows, cols].astype(F32) + jnp.dot(mixed[layer, rows, :], wo_buf[n], preferred_element_type=F32)
+            added = rows_x[rows, cols].astype(F32) + jnp.dot(mixed[rows, :], wo_buf[n], preferred_element_type=F32)
             acc[:count, cols] = added.astype(BF16).astype(F32)
-        if chunk == 1:
-            @pl.when(layer < last)
-            def _():
-                for n in range(tiles):
-                    wo_copy(layer + 1, n).start()
-
-        normalize(lambda r: acc[r, :], row0, count, gain_mlp[layer])
+        normalize(lambda r: acc[r, :], row0, count, gain_of(gain_mlp, layer))
 
         def step_at(k):
             return k if chunk == 0 else ff_steps - 1 - k
@@ -463,10 +475,6 @@
                 def _():
                     start(layer, step - FF_SLOTS)
 
-                @pl.when((step < FF_SLOTS) & (layer < last))
-                def _():
-                    start(layer + 1, step)
-
         def start_gu(which, step):
             for copy in gu_copies(which, step):
                 copy.start()
@@ -487,32 +495,30 @@
         if between is None:
             lax.fori_loop(1, ff_steps, body, 0)
         else:
-            lax.fori_loop(1, SPLIT, body, 0)
+            split = jnp.where(layer == 0, SPLIT[0], SPLIT[1])
+            lax.fori_loop(1, split, body, 0)
             between()
-            lax.fori_loop(SPLIT, ff_steps, body, 0)
+            lax.fori_loop(split, ff_steps, body, 0)
         narrow(ff_steps - 1)
         refill(ff_steps - 1, start_down)
         rows_x[rows, :] = acc[:count].astype(BF16)
 
+    scope = jax.named_scope
     pltpu.make_async_copy(x_in, rows_x.at[0:2 * blk], sem_x).start()
-    for r in range(tiles):
+    barrier = pltpu.get_barrier_semaphore()
+    for i in range(1, group):
+        pl.semaphore_signal(barrier, inc=1, device_id={"cp": lax.rem(me + i, group)}, device_id_type=MESH)
+    qkv_copy(0, order_a[0], 0).start()
+    dec_h[...] = jnp.zeros_like(dec_h)
+    pltpu.make_async_copy(x_in, rows_x.at[0:2 * blk], sem_x).wait()
+    for r in range(1, tiles):
         qkv_copy(0, order_a[0], r).start()
     for tensor in range(3):
         dec_copy(0, tensor).start()
-    for n in range(tiles):
-        wo_copy(0, n).start()
-    for step in range(FF_SLOTS):
-        for copy in gu_copies(0, step):
-            copy.start()
-        down_copy(0, step).start()
-
-    barrier = pltpu.get_barrier_semaphore()
-    for i in range(1, group):
-        pl.semaphore_signal(barrier, inc=1, device_id={"cp": lax.rem(me + i, group)}, device_id_type=MESH)
-    dec_h[...] = jnp.zeros_like(dec_h)
-    pltpu.make_async_copy(x_in, rows_x.at[0:2 * blk], sem_x).wait()
-    normalize_x(0, 2 * blk, gain_attn[0])
-    pl.semaphore_wait(barrier, others)
+    with scope("norm_first"):
+        normalize_x(0, 2 * blk, gain_of(gain_attn, 0))
+    with scope("barrier"):
+        pl.semaphore_wait(barrier, others)
 
     my_cols = pl.ds(pl.multiple_of(me * LANES, LANES), LANES)
 
@@ -524,20 +530,32 @@
 
     lax.fori_loop(0, others, part_out, 0)
     emb_part[me] = emb_in[:, my_cols]
-    project(0, 0)
-    wait_recv(emb_part.at[0:others], recv_e)
-    emb_sum[...] = jnp.sum(emb_part[...].astype(F32), axis=0).astype(BF16)
-    emb_full[:, my_cols] = emb_sum[...]
-
-    def sum_out(i, carry):
-        device = lax.rem(me + 1 + i, group)
-        remote(emb_sum, emb_full.at[:, my_cols], send_f, recv_f, device).start()
-        return carry
-
-    lax.fori_loop(0, others, sum_out, 0)
+    def sum_looked_up():
+        with scope("embed"):
+            wait_recv(emb_part.at[0:others], recv_e)
+            emb_sum[...] = jnp.sum(emb_part[...].astype(F32), axis=0).astype(BF16)
+            emb_full[:, my_cols] = emb_sum[...]
+
+            def sum_out(i, carry):
+                device = lax.rem(me + 1 + i, group)
+                remote(emb_sum, emb_full.at[:, my_cols], send_f, recv_f, device).start()
+                return carry
+
+            lax.fori_loop(0, others, sum_out, 0)
+
+    with scope("project_first"):
+        project(0, 0, sum_looked_up)
 
     def layer_body(layer, carry):
-        project(layer, 1)
+        with scope("project_b"):
+            project(layer, 1)
+
+        for n in range(tiles):
+            wo_copy(layer, n).start()
+        for step in range(FF_SLOTS):
+            for copy in gu_copies(layer, step):
+                copy.start()
+            down_copy(layer, step).start()
 
         @pl.when(layer == 0)
         def _():
@@ -545,53 +563,66 @@
             rows_x[2 * blk:2 * blk + PAD] = emb_full[...]
             wide = emb_full[...].astype(F32)
             inv = lax.rsqrt(jnp.mean(wide * wide, axis=-1, keepdims=True) + NORM_EPS)
-            rows_h[2 * blk:2 * blk + PAD] = (wide * inv * gain_attn[0]).astype(BF16)
-
-        project_decode(layer)
-        for tensor in range(3):
-            wait_recv(got.at[layer, tensor, 0:others], recv_qkv.at[layer, 0, tensor])
-        turn_keys(layer, 0)
-        save_cache(layer, 0)
-        attend_triangle(layer, 0)
-        send_all(layer, 1, 1)
-        send_all(layer, 2, 1)
-        wait_recv(got.at[layer, 0, 0:others], recv_qkv.at[layer, 1, 0])
-        attend_square(layer)
-        for tensor in range(3):
-            wait_send(sent.at[tensor, 0, 0:others], send_qkv.at[0, tensor])
-        wait_recv(mixed_sent.at[0:others], recv_o.at[layer, 0])
+            rows_h[2 * blk:2 * blk + PAD] = (wide * inv * gain_of(gain_attn, 0)).astype(BF16)
+
+        with scope("project_dec"):
+            project_decode(layer)
+        with scope("wait_a"):
+            for tensor in range(3):
+                wait_recv(home(layer, tensor).at[0:others], recv_qkv.at[layer, 0, tensor])
+        with scope("attend_aa"):
+            turn_keys(layer, 0)
+            save_cache(layer, 0)
+            attend_triangle(layer, 0)
+        send_rest(layer)
+        with scope("wait_q"):
+            wait_recv(got_q.at[0:others], recv_qkv.at[layer, 1, 0])
+        with scope("attend_ba"):
+            attend_square(layer)
+        with scope("wait_oa"):
+            for tensor in range(3):
+                wait_send(sent.at[tensor, 0, 0:others], send_qkv.at[0, tensor])
+            wait_recv(mixed_sent.at[0:others], recv_o.at[layer, 0])
 
         def finish_attention():
-            for tensor in (1, 2):
-                wait_recv(got.at[layer, tensor, 0:others], recv_qkv.at[layer, 1, tensor])
-            turn_keys(layer, 1)
-            attend_triangle(layer, 1)
-            attend_decode(layer)
-            save_cache(layer, 1)
-
-        dense(layer, 0, finish_attention)
-        for tensor in range(3):
-            wait_send(sent.at[tensor, 1, 0:others], send_qkv.at[1, tensor])
-        wait_send(mixed_sent.at[0:others], send_o.at[0])
+            with scope("wait_kv"):
+                wait_recv(got.at[layer, pl.ds(0, 2), pl.ds(0, others)], recv_qkv.at[layer, 1, 1])
+            wait_send(mixed_sent.at[0:others], send_o.at[0])
+            with scope("attend_bb"):
+                turn_keys(layer, 1)
+                attend_triangle(layer, 1)
+            with scope("attend_dec"):
+                attend_decode(layer)
+                save_cache(layer, 1)
+
+        with scope("dense_a"):
+            dense(layer, 0, finish_attention)
+        with scope("drain_a"):
+            wait_send(sent.at[0, 1, 0:others], send_qkv.at[1, 0])
+            wait_send(sent.at[pl.ds(1, 2), 1, pl.ds(0, others)], send_qkv.at[1, 1])
 
         @pl.when(layer < last)
         def _():
-            normalize_x(0, blk, gain_attn[layer + 1])
-            project(layer + 1, 0)
+            with scope("project_a"):
+                normalize_x(0, blk, gain_of(gain_attn, layer + 1))
+                project(layer + 1, 0)
 
         @pl.when(layer == last)
         def _():
             pltpu.make_async_copy(rows_x.at[0:blk], x_out.at[0:blk], sem_out.at[0]).start()
 
-        wait_recv(mixed_sent.at[0:others], recv_o.at[layer, 1])
-        wait_recv(emb_part.at[0:others], recv_d.at[layer])
-        dense(layer, 1, None)
-        wait_send(mixed_sent.at[0:others], send_o.at[1])
-        wait_send(emb_part.at[0:others], send_d)
+        with scope("wait_ob"):
+            wait_recv(mixed_sent.at[0:others], recv_o.at[layer, 1])
+            wait_recv(emb_part.at[0:others], recv_d.at[layer])
+        with scope("dense_b"):
+            dense(layer, 1, None)
+        with scope("drain_b"):
+            wait_send(mixed_sent.at[0:others], send_o.at[1])
+            wait_send(emb_part.at[0:others], send_d)
 
         @pl.when(layer < last)
         def _():
-            normalize_x(blk, b_rows, gain_attn[layer + 1])
+            normalize_x(blk, b_rows, gain_of(gain_attn, layer + 1))
 
         return carry
 
@@ -607,6 +638,35 @@
     for part in range(2):
         where = pl.ds(part * blk, blk)
         pltpu.make_async_copy(rows_x.at[where], x_out.at[where], sem_out.at[part]).wait()
+
+
+def place_kernel(x_ref, k_ref, v_ref, dec_ref, x_to, k_to, v_to, dec_to, x_held, k_held, v_held, dec_held, sems):
+    moves = ((k_ref, k_held, k_to), (v_ref, v_held, v_to), (x_ref, x_held, x_to))
+    for n, (source, held, _) in enumerate(moves):
+        pltpu.make_async_copy(source, held, sems.at[0, n]).start()
+    pltpu.make_async_copy(dec_ref, dec_held, sems.at[0, 3]).start()
+    for n, (source, held, result) in enumerate(moves):
+        pltpu.make_async_copy(source, held, sems.at[0, n]).wait()
+        pltpu.make_async_copy(held, result, sems.at[1, n]).start()
+    pltpu.make_async_copy(dec_ref, dec_held, sems.at[0, 3]).wait()
+    dec_to[...] = dec_held[0:dec_to.shape[0]]
+    for n, (_, held, result) in enumerate(moves):
+        pltpu.make_async_copy(held, result, sems.at[1, n]).wait()
+
+
+def place(steps, *arrays):
+    spec = pl.BlockSpec(memory_space=pl.ANY)
+    shapes = [jax.ShapeDtypeStruct(a.shape, a.dtype) for a in arrays]
+    shapes[-1] = jax.ShapeDtypeStruct((steps,) + arrays[-1].shape[1:], arrays[-1].dtype)
+    return pl.pallas_call(
+        place_kernel,
+        out_shape=tuple(shapes),
+        in_specs=[spec] * len(arrays),
+        out_specs=(spec, spec, spec, pl.BlockSpec(memory_space=pltpu.VMEM)),
+        scratch_shapes=[pltpu.VMEM(a.shape, a.dtype) for a in arrays] + [pltpu.SemaphoreType.DMA((2, len(arrays)))],
+        compiler_params=pltpu.CompilerParams(vmem_limit_bytes=67_000_000),
+        name="place",
+    )(*arrays)
 
 
 def solution(mesh):
@@ -645,11 +705,12 @@
         scratch = [
             pltpu.VMEM((2 * blk + PAD, d_model), BF16),
             pltpu.VMEM((2 * blk + PAD, d_model), BF16),
-            pltpu.VMEM((num_layers, 2 * blk + PAD, d_model), BF16),
+            pltpu.VMEM((2 * blk + PAD, d_model), BF16),
             pltpu.VMEM((3, 2, group, LANES, blk), BF16),
-            pltpu.VMEM((num_layers, 3, 2 * group, LANES, blk), BF16),
+            pltpu.VMEM((2 * group, LANES, blk), BF16),
+            pltpu.VMEM((num_layers, 2, 2 * group, LANES, blk), BF16),
             pltpu.VMEM((seq_len, LANES), BF16),
-            pltpu.VMEM((2 * group, blk, LANES), BF16),
+            pltpu.VMEM((group, blk, LANES), BF16),
             pltpu.VMEM((2, 2 * heads_dev, KEY_TILE, quarter), F32),
             pltpu.VMEM((2, 2 * heads_dev, 1, quarter), F32),
             pltpu.VMEM((pairs, 2 * heads_dev, 1, quarter), F32),
@@ -685,10 +746,10 @@
             in_specs=[any_spec, vmem, vmem, vmem, vmem] + [any_spec] * 7,
             out_specs=(any_spec, any_spec, any_spec, vmem),
             scratch_shapes=scratch,
-            compiler_params=pltpu.CompilerParams(collective_id=0, has_side_effects=True, vmem_limit_bytes=66_000_000),
+            compiler_params=pltpu.CompilerParams(collective_id=0, has_side_effects=True, vmem_limit_bytes=67_000_000),
             name="prefill_decode",
         )(
-            x_rows, emb, norm_attn.astype(F32)[:, None, :], norm_mlp.astype(F32)[:, None, :], tables,
+            x_rows, emb, norm_attn, norm_mlp, tables,
             head_rows(w_q), head_rows(w_k), head_rows(w_v), w_o.reshape(num_layers * d_model, d_model),
             w_gate.reshape(num_layers * d_model, ff_dim), w_up.reshape(num_layers * d_model, ff_dim), w_down.reshape(num_layers * ff_dim, d_model),
         )
@@ -696,7 +757,8 @@
         def cache(flat):
             return flat.reshape(num_layers, heads_dev, head_dim, seq_len).transpose(0, 3, 1, 2)
 
-        return x_new, cache(k_flat), cache(v_flat), dec[:steps]
+        x_new, k_flat, v_flat, dec = place(steps, x_new, k_flat, v_flat, dec)
+        return x_new, cache(k_flat), cache(v_flat), dec
 
     replicated = P()
     in_specs = (P(("req", "cp"), None), P("req"), P("cp", None)) + (replicated,) * 9

time: 290 us -> 259 us (0.89)
  Pallas kernels: 277 us -> 259 us
  local copies, waits for them, and re-layouts: 12.6 us -> 0 us
    pallas_call x1, Pallas kernels: 275 us -> 252 us  [local_program(): pl.pallas_call(functools.partial(main_kernel, group, head_dim, num_layers...]
    unnamed x3 -> x0, local copies, waits for them, and re-layouts: 8.56 us -> none
    pallas_call x0 -> x1, Pallas kernels: none -> 4.62 us  [place(): pl.pallas_call(place_kernel, out_shape=tuple(shapes), in_specs=[spec] * l...]
where the time goes in v2:
time: 259 us; the launch traced here: 261 us
  Pallas kernels  259 us (100%)
    pallas_call x1, Pallas kernels, local_program(): pl.pallas_call(functools.partial(main_kernel, group, head_dim, num_layers...  252 us

profile of v2, /device:TPU:23, one launch (start us, length us, event | category | flops | bytes accessed | tf_op | source)
XLA Modules:
  0.0 261.0 jit_solution(14667862132133246736)
XLA Ops:
  0.7 2.3 pick_rows.1.emb_in
  3.0 0.3 multiply_cosine_fusion
  3.2 0.7 pad_maximum_fusion
  3.9 252.3 %prefill_decode.1 = (bf16[256,2048]{1,0:T(8,128)(2,1)}, bf16[2,128,4096]{2,1,0:T(8,128)(2,1)}, bf16[2,128,4096]{2,1,0:T(8,128)(2,1)}, bf16[16,2048]{1,0:T(8,128)(2,1)}) custom-call(bf16[256,2048]{1,0:T(8,128)(2,1)} %x_in.1, bf16[16,2048]{1,0:T(8,128)(2,1)} %pick_rows.1.emb_in, bf16[2,2048]{1,0:T(2,128)(2,1)} %gain_attn.1, bf16[2,2048]{1,0:T(2,128)(2,1)} %gain_mlp.1, ...), custom_call_target="tpu_custom_call" | custom-call | tf_op jit(solution)/shard_map/prefill_decode/pallas_call | solution.py:738
  256.2 4.6 %place.1 = (bf16[256,2048]{1,0:T(8,128)(2,1)}, bf16[2,128,4096]{2,1,0:T(8,128)(2,1)}, bf16[2,128,4096]{2,1,0:T(8,128)(2,1)}, bf16[4,2048]{1,0:T(4,128)(2,1)}) custom-call(bf16[256,2048]{1,0:T(8,128)(2,1)} %get-tuple-element.12.x_ref, bf16[2,128,4096]{2,1,0:T(8,128)(2,1)} %get-tuple-element.13.k_ref, bf16[2,128,4096]{2,1,0:T(8,128)(2,1)} %get-tuple-element.14.v_ref, ...), custom_call_target="tpu_custom_call" | custom-call | tf_op jit(solution)/shard_map/place/pallas_call | solution.py:661
  (4 shorter events, 0.0 us)

commit v3 on v2

--- a/solution.py
+++ b/solution.py
@@ -22,9 +22,9 @@
 SPLIT = (14, 12)
 
 
-def pick_kernel(vocab_dev, ids_ref, base_ref, table_ref, out_ref, rows, sems):
+def pick_kernel(vocab_dev, ids_ref, table_ref, out_ref, rows, sems):
     steps = ids_ref.shape[0]
-    base = base_ref[0]
+    base = lax.axis_index("cp") * vocab_dev
 
     def copy(t):
         local = jnp.clip(ids_ref[t] - base, 0, vocab_dev - 1)
@@ -46,7 +46,7 @@
     out_ref[...] = jnp.concatenate(picked, axis=0).astype(BF16)
 
 
-def pick_rows(token_ids, base, table_rows):
+def pick_rows(token_ids, table_rows):
     vocab_dev, d_model = table_rows.shape
     steps = token_ids.shape[0]
     return pl.pallas_call(
@@ -54,13 +54,12 @@
         out_shape=jax.ShapeDtypeStruct((PAD, d_model), BF16),
         in_specs=[
             pl.BlockSpec(memory_space=pltpu.SMEM),
-            pl.BlockSpec(memory_space=pltpu.SMEM),
             pl.BlockSpec(memory_space=pl.ANY),
         ],
         out_specs=pl.BlockSpec(memory_space=pltpu.VMEM),
         scratch_shapes=[pltpu.VMEM((steps, 8, d_model), BF16), pltpu.SemaphoreType.DMA((steps,))],
         name="pick_rows",
-    )(token_ids, base, table_rows)
+    )(token_ids, table_rows)
 
 
 def main_kernel(
@@ -68,7 +67,7 @@
     x_in, emb_in, gain_attn, gain_mlp, tables, w_q, w_k, w_v, w_o, w_gate, w_up, w_down,
     x_out, k_cache, v_cache, dec_out,
     rows_x, rows_h, mixed, sent, got_q, got, key_rows, mixed_sent, score, best, run_max, run_acc,
-    qkv_ring, wo_buf, gate_ring, up_ring, down_ring, dec_w, dec_h, dec_q, dec_k, dec_v, acc, gated, emb_part, emb_full, emb_sum, dec_sent,
+    qkv_ring, wo_buf, gate_ring, up_ring, down_ring, dec_w, dec_q, dec_k, dec_v, acc, gated, emb_part, emb_sum, dec_sent,
     sem_x, sem_qkv, sem_wo, sem_ff, sem_dec, send_qkv, recv_qkv, send_o, recv_o, send_d, recv_d, send_e, recv_e, send_f, recv_f, sem_cache, sem_out,
 ):
     me = lax.axis_index("cp")
@@ -195,7 +194,7 @@
         turned = jnp.concatenate([first * cosines - second * sines, second * cosines + first * sines], axis=1)
         return turned.reshape(flat.shape)
 
-    def project(layer, chunk, after_first=None):
+    def project(layer, chunk, between=()):
         order = order_a if chunk == 0 else order_a[::-1]
         for place, tensor in enumerate(order):
             def body(i, carry, place=place, tensor=tensor):
@@ -227,15 +226,16 @@
             home(layer, tensor)[block_of(chunk, me)] = sent[tensor, chunk, me]
             if chunk == 1 and tensor == 0:
                 send_queries(layer)
-            if place == 0 and after_first is not None:
-                after_first()
+            if place < len(between):
+                between[place]()
 
     def project_decode(layer):
-        dec_h[0:PAD] = rows_h[2 * blk:2 * blk + PAD]
-        dec_h[head_dim:head_dim + PAD] = rows_h[2 * blk:2 * blk + PAD]
+        few = rows_h[2 * blk:2 * blk + PAD]
+        blank = jnp.zeros((head_dim - PAD, d_model), BF16)
+        normed = jnp.concatenate([few, blank] * heads_dev, axis=0)
         for tensor in range(3):
             dec_copy(layer, tensor).wait()
-            flat = lax.dot_general(dec_w[tensor], dec_h[...], (((1,), (1,)), ((), ())), preferred_element_type=F32)
+            flat = lax.dot_general(dec_w[tensor], normed, (((1,), (1,)), ((), ())), preferred_element_type=F32)
             if tensor != 2:
                 flat = rotate(flat, 2)
             if tensor == 0:
@@ -325,28 +325,29 @@
                 mixed_sent[pair_blocks * place + 2 * u + i] = turned[i * blk:(i + 1) * blk]
 
     def hand_out(layer, chunk, place):
-        mine = pl.ds(pl.multiple_of(me * LANES, LANES), LANES)
         for i in range(pair_blocks):
             j = pair_blocks * place + i
             device = j if chunk == 0 else group - 1 - j
-            where = mixed.at[chunk * blk:(chunk + 1) * blk, mine]
+            where = mixed.at[me, chunk * blk:(chunk + 1) * blk]
             send_to(remote(mixed_sent.at[j], where, send_o.at[chunk], recv_o.at[layer, chunk], device), device)
 
             @pl.when(device == me)
             def _(j=j):
-                mixed[chunk * blk:(chunk + 1) * blk, mine] = mixed_sent[j]
-
-    def attend_triangle(layer, chunk):
+                mixed[me, chunk * blk:(chunk + 1) * blk] = mixed_sent[j]
+
+    def attend_triangle(layer, chunk, middle=None):
         base = chunk * pairs
-        turn = me // (group // pairs)
+        quarter = me // (group // pairs)
+        turn = lax.rem(quarter + 1 if chunk == 0 else pairs - quarter, pairs)
         first_slot = [0]
         for pair in range(pairs - 1):
             first_slot.append((first_slot[-1] + pair + 1) % 2)
 
-        def one_pair(pair):
+        def one_pair(pair, i):
             slot = first_slot[pair]
+            then = jnp.where(i == pairs - 1, pair, (pair + 1) % pairs)
             for tile in range(pair + 1):
-                after = (pair, tile + 1) if tile < pair else ((pair + 1) % pairs, 0)
+                after = (pair, tile + 1) if tile < pair else (then, 0)
                 scores(layer, base + after[0], base + after[1], 1 - slot)
                 if tile == pair:
                     mask_diagonal(slot)
@@ -364,7 +365,9 @@
             for pair in range(pairs):
                 @pl.when(lax.rem(turn + i, pairs) == pair)
                 def _(pair=pair):
-                    one_pair(pair)
+                    one_pair(pair, i)
+            if middle is not None:
+                pl.when(i == pairs // 2 - 1)(middle)
             return carry
 
         lax.fori_loop(0, pairs, body, 0)
@@ -379,6 +382,11 @@
                 else:
                     scores(layer, pairs + jnp.minimum(pair + 1, pairs - 1), 0, 0)
                 absorb(layer, tile, tile % 2, pair, first=tile == 0)
+
+            @pl.when(pair == jnp.where(layer == 0, pairs - 1, pairs - 2))
+            def _():
+                send_rest(layer)
+
             return carry
 
         lax.fori_loop(0, pairs, body, 0)
@@ -386,22 +394,22 @@
     def attend_decode(layer):
         ones = jnp.ones((PAD, KEY_TILE), BF16)
         queries = dec_q[...]
-        wide = slice(0, LANES)
-        spots = [(i // score.shape[1], i % score.shape[1]) for i in range(blocks // pair_blocks)]
         value = jnp.dot(dec_k[...], queries, preferred_element_type=F32)
         key = lax.broadcasted_iota(jnp.int32, value.shape, 0)
         query = lax.rem(lax.broadcasted_iota(jnp.int32, value.shape, 1), head_dim)
         value = jnp.where((key <= query) & (key < steps), value, -jnp.inf)
         top = jnp.max(value, axis=0, keepdims=True)
-        for tile, (i, j) in enumerate(spots):
-            old = jnp.dot(key_rows[tile * KEY_TILE:(tile + 1) * KEY_TILE, :], queries, preferred_element_type=F32)
-            score[i, j, :, wide] = old
-            top = jnp.maximum(top, jnp.max(old, axis=0, keepdims=True))
+
+        def old(tile):
+            return jnp.dot(key_rows[tile * KEY_TILE:(tile + 1) * KEY_TILE, :], queries, preferred_element_type=F32)
+
+        for tile in range(blocks // pair_blocks):
+            top = jnp.maximum(top, jnp.max(old(tile), axis=0, keepdims=True))
         held = jnp.concatenate([dec_v[...], ones[:, :LANES]], axis=0)
         total = jnp.dot(held, jnp.exp2((value - top) * exp_scale).astype(BF16), preferred_element_type=F32)
-        for tile, (i, j) in enumerate(spots):
+        for tile in range(blocks // pair_blocks):
             held = jnp.concatenate([got[layer, 1, tile * pair_blocks + k] for k in range(pair_blocks)], axis=1)
-            probs = jnp.exp2((score[i, j, :, wide] - top) * exp_scale).astype(BF16)
+            probs = jnp.exp2((old(tile) - top) * exp_scale).astype(BF16)
             total = total + jnp.dot(jnp.concatenate([held, ones], axis=0), probs, preferred_element_type=F32)
         turned = (total[:LANES] / total[LANES:LANES + 1]).T
         lane = lax.broadcasted_iota(jnp.int32, (PAD, LANES), 1)
@@ -409,12 +417,11 @@
         for h in range(1, heads_dev):
             result = jnp.where(lane >= h * head_dim, turned[h * head_dim:h * head_dim + PAD], result)
         dec_sent[...] = result.astype(BF16)
-        mine = pl.ds(pl.multiple_of(me * LANES, LANES), LANES)
-        mixed[2 * blk:2 * blk + PAD, mine] = dec_sent[...]
+        mixed[me, 2 * blk:2 * blk + PAD] = dec_sent[...]
 
         def send(i, carry):
             device = lax.rem(me + 1 + i, group)
-            remote(dec_sent, mixed.at[2 * blk:2 * blk + PAD, mine], send_d, recv_d.at[layer], device).start()
+            remote(dec_sent, mixed.at[me, 2 * blk:2 * blk + PAD], send_d, recv_d.at[layer], device).start()
             return carry
 
         lax.fori_loop(0, others, send, 0)
@@ -422,11 +429,12 @@
     def dense(layer, chunk, between):
         row0, count = (0, blk) if chunk == 0 else (blk, b_rows)
         rows = slice(row0, row0 + count)
+        heads = jnp.concatenate([mixed[n, rows] for n in range(group)], axis=1)
         for n in range(tiles):
             if chunk == 0:
                 wo_copy(layer, n).wait()
             cols = slice(n * QKV_ROWS, (n + 1) * QKV_ROWS)
-            added = rows_x[rows, cols].astype(F32) + jnp.dot(mixed[rows, :], wo_buf[n], preferred_element_type=F32)
+            added = rows_x[rows, cols].astype(F32) + jnp.dot(heads, wo_buf[n], preferred_element_type=F32)
             acc[:count, cols] = added.astype(BF16).astype(F32)
         normalize(lambda r: acc[r, :], row0, count, gain_of(gain_mlp, layer))
 
@@ -509,42 +517,44 @@
     for i in range(1, group):
         pl.semaphore_signal(barrier, inc=1, device_id={"cp": lax.rem(me + i, group)}, device_id_type=MESH)
     qkv_copy(0, order_a[0], 0).start()
-    dec_h[...] = jnp.zeros_like(dec_h)
     pltpu.make_async_copy(x_in, rows_x.at[0:2 * blk], sem_x).wait()
     for r in range(1, tiles):
         qkv_copy(0, order_a[0], r).start()
     for tensor in range(3):
         dec_copy(0, tensor).start()
     with scope("norm_first"):
-        normalize_x(0, 2 * blk, gain_of(gain_attn, 0))
+        normalize_x(0, blk, gain_of(gain_attn, 0))
     with scope("barrier"):
         pl.semaphore_wait(barrier, others)
 
     my_cols = pl.ds(pl.multiple_of(me * LANES, LANES), LANES)
 
-    def part_out(i, carry):
-        device = lax.rem(me + 1 + i, group)
-        cols = pl.ds(pl.multiple_of(device * LANES, LANES), LANES)
-        remote(emb_in.at[:, cols], emb_part.at[me], send_e, recv_e, device).start()
-        return carry
-
-    lax.fori_loop(0, others, part_out, 0)
-    emb_part[me] = emb_in[:, my_cols]
+    def split_looked_up():
+        def part_out(i, carry):
+            device = lax.rem(me + 1 + i, group)
+            cols = pl.ds(pl.multiple_of(device * LANES, LANES), LANES)
+            remote(emb_in.at[:, cols], emb_part.at[me], send_e, recv_e, device).start()
+            return carry
+
+        lax.fori_loop(0, others, part_out, 0)
+        emb_part[me] = emb_in[:, my_cols]
+
     def sum_looked_up():
         with scope("embed"):
             wait_recv(emb_part.at[0:others], recv_e)
             emb_sum[...] = jnp.sum(emb_part[...].astype(F32), axis=0).astype(BF16)
-            emb_full[:, my_cols] = emb_sum[...]
+            rows_x[2 * blk:2 * blk + PAD, my_cols] = emb_sum[...]
 
             def sum_out(i, carry):
                 device = lax.rem(me + 1 + i, group)
-                remote(emb_sum, emb_full.at[:, my_cols], send_f, recv_f, device).start()
+                remote(emb_sum, rows_x.at[2 * blk:2 * blk + PAD, my_cols], send_f, recv_f, device).start()
                 return carry
 
             lax.fori_loop(0, others, sum_out, 0)
 
     with scope("project_first"):
-        project(0, 0, sum_looked_up)
+        project(0, 0, (split_looked_up, sum_looked_up))
+        normalize_x(blk, blk, gain_of(gain_attn, 0))
 
     def layer_body(layer, carry):
         with scope("project_b"):
@@ -560,13 +570,12 @@
         @pl.when(layer == 0)
         def _():
             wait_recv(emb_part.at[0:others], recv_f)
-            rows_x[2 * blk:2 * blk + PAD] = emb_full[...]
-            wide = emb_full[...].astype(F32)
+            wide = rows_x[2 * blk:2 * blk + PAD].astype(F32)
             inv = lax.rsqrt(jnp.mean(wide * wide, axis=-1, keepdims=True) + NORM_EPS)
             rows_h[2 * blk:2 * blk + PAD] = (wide * inv * gain_of(gain_attn, 0)).astype(BF16)
-
-        with scope("project_dec"):
-            project_decode(layer)
+            with scope("project_dec"):
+                project_decode(layer)
+
         with scope("wait_a"):
             for tensor in range(3):
                 wait_recv(home(layer, tensor).at[0:others], recv_qkv.at[layer, 0, tensor])
@@ -574,7 +583,6 @@
             turn_keys(layer, 0)
             save_cache(layer, 0)
             attend_triangle(layer, 0)
-        send_rest(layer)
         with scope("wait_q"):
             wait_recv(got_q.at[0:others], recv_qkv.at[layer, 1, 0])
         with scope("attend_ba"):
@@ -585,14 +593,18 @@
             wait_recv(mixed_sent.at[0:others], recv_o.at[layer, 0])
 
         def finish_attention():
+            @pl.when(layer > 0)
+            def _():
+                with scope("project_dec"):
+                    project_decode(layer)
+
             with scope("wait_kv"):
                 wait_recv(got.at[layer, pl.ds(0, 2), pl.ds(0, others)], recv_qkv.at[layer, 1, 1])
             wait_send(mixed_sent.at[0:others], send_o.at[0])
             with scope("attend_bb"):
                 turn_keys(layer, 1)
-                attend_triangle(layer, 1)
+                attend_triangle(layer, 1, lambda: attend_decode(layer))
             with scope("attend_dec"):
-                attend_decode(layer)
                 save_cache(layer, 1)
 
         with scope("dense_a"):
@@ -684,7 +696,7 @@
         heads_dev = num_heads // group
         assert heads_dev * head_dim == LANES and kv_heads == num_heads and blk == LANES
 
-        emb = pick_rows(token_ids, (device * table_rows.shape[0]).reshape(1), table_rows)
+        emb = pick_rows(token_ids, table_rows)
 
         offsets = jnp.arange(LANES, dtype=jnp.int32)
         positions = jnp.stack([device * blk + offsets, (2 * group - 1 - device) * blk + offsets, seq_len + offsets % head_dim])
@@ -705,7 +717,7 @@
         scratch = [
             pltpu.VMEM((2 * blk + PAD, d_model), BF16),
             pltpu.VMEM((2 * blk + PAD, d_model), BF16),
-            pltpu.VMEM((2 * blk + PAD, d_model), BF16),
+            pltpu.VMEM((group, 2 * blk + PAD, LANES), BF16),
             pltpu.VMEM((3, 2, group, LANES, blk), BF16),
             pltpu.VMEM((2 * group, LANES, blk), BF16),
             pltpu.VMEM((num_layers, 2, 2 * group, LANES, blk), BF16),
@@ -721,14 +733,12 @@
             pltpu.VMEM((FF_SLOTS, d_model, FF_TILE), BF16),
             pltpu.VMEM((FF_SLOTS, FF_TILE, d_model), BF16),
             pltpu.VMEM((3, LANES, d_model), BF16),
-            pltpu.VMEM((LANES, d_model), BF16),
             pltpu.VMEM((LANES, LANES), BF16),
             pltpu.VMEM((LANES, LANES), BF16),
             pltpu.VMEM((LANES, LANES), BF16),
             pltpu.VMEM((blk + PAD, d_model), F32),
             pltpu.VMEM((blk + PAD, FF_TILE), BF16),
             pltpu.VMEM((group, PAD, LANES), BF16),
-            pltpu.VMEM((PAD, d_model), BF16),
             pltpu.VMEM((PAD, LANES), BF16),
             pltpu.VMEM((PAD, LANES), BF16),
             dma, dma((tiles,)), dma((tiles,)), dma((3, FF_SLOTS)), dma((3,)),

time: 259 us -> 254 us (0.981); the launches traced: 261 us -> 252 us
  Pallas kernels: 259 us -> 250 us
    pallas_call x1, Pallas kernels: 252 us -> 243 us  [local_program(): pl.pallas_call(functools.partial(main_kernel, group, head_dim, num_layers...]
where the time goes in v3:
time: 254 us; the launch traced here: 252 us
  Pallas kernels  250 us (98%)
    pallas_call x1, Pallas kernels, local_program(): pl.pallas_call(functools.partial(main_kernel, group, head_dim, num_layers...  243 us

profile of v3, /device:TPU:23, one launch (start us, length us, event | category | flops | bytes accessed | tf_op | source)
XLA Modules:
  0.0 251.6 jit_solution(11022108946126203419)
XLA Ops:
  0.7 2.3 pick_rows.1.emb_in
  3.0 0.3 multiply_cosine_fusion
  3.2 0.7 pad_maximum_fusion
  3.9 242.9 %prefill_decode.1 = (bf16[256,2048]{1,0:T(8,128)(2,1)}, bf16[2,128,4096]{2,1,0:T(8,128)(2,1)}, bf16[2,128,4096]{2,1,0:T(8,128)(2,1)}, bf16[16,2048]{1,0:T(8,128)(2,1)}) custom-call(bf16[256,2048]{1,0:T(8,128)(2,1)} %x_in.1, bf16[16,2048]{1,0:T(8,128)(2,1)} %pick_rows.1.emb_in, bf16[2,2048]{1,0:T(2,128)(2,1)} %gain_attn.1, bf16[2,2048]{1,0:T(2,128)(2,1)} %gain_mlp.1, ...), custom_call_target="tpu_custom_call" | custom-call | tf_op jit(solution)/shard_map/prefill_decode/pallas_call | solution.py:748
  246.8 4.6 %place.1 = (bf16[256,2048]{1,0:T(8,128)(2,1)}, bf16[2,128,4096]{2,1,0:T(8,128)(2,1)}, bf16[2,128,4096]{2,1,0:T(8,128)(2,1)}, bf16[4,2048]{1,0:T(4,128)(2,1)}) custom-call(bf16[256,2048]{1,0:T(8,128)(2,1)} %get-tuple-element.12.x_ref, bf16[2,128,4096]{2,1,0:T(8,128)(2,1)} %get-tuple-element.13.k_ref, bf16[2,128,4096]{2,1,0:T(8,128)(2,1)} %get-tuple-element.14.v_ref, ...), custom_call_target="tpu_custom_call" | custom-call | tf_op jit(solution)/shard_map/place/pallas_call | solution.py:673
  (4 shorter events, 0.0 us)

commit v4 on v3

--- a/solution.py
+++ b/solution.py
@@ -64,7 +64,7 @@
 
 def main_kernel(
     group, head_dim, num_layers, steps,
-    x_in, emb_in, gain_attn, gain_mlp, tables, w_q, w_k, w_v, w_o, w_gate, w_up, w_down,
+    x_in, emb_in, gain_attn, gain_mlp, cos_tab, sin_tab, w_q, w_k, w_v, w_o, w_gate, w_up, w_down,
     x_out, k_cache, v_cache, dec_out,
     rows_x, rows_h, mixed, sent, got_q, got, key_rows, mixed_sent, score, best, run_max, run_acc,
     qkv_ring, wo_buf, gate_ring, up_ring, down_ring, dec_w, dec_q, dec_k, dec_v, acc, gated, emb_part, emb_sum, dec_sent,
@@ -188,7 +188,7 @@
         normalize(read, row0, count, gain)
 
     def rotate(flat, which):
-        cosines, sines = tables[2 * which], tables[2 * which + 1]
+        cosines, sines = cos_tab[which], sin_tab[which]
         heads = flat.reshape(flat.shape[0] // head_dim, head_dim, flat.shape[1])
         first, second = heads[:, :half], heads[:, half:]
         turned = jnp.concatenate([first * cosines - second * sines, second * cosines + first * sines], axis=1)
@@ -702,8 +702,6 @@
         positions = jnp.stack([device * blk + offsets, (2 * group - 1 - device) * blk + offsets, seq_len + offsets % head_dim])
         inv_freq = 1.0 / (ROPE_BASE ** (jnp.arange(0, head_dim, 2, dtype=F32) / head_dim))
         angles = positions.astype(F32)[:, None, :] * inv_freq[None, :, None]
-        tables = jnp.stack([jnp.cos(angles), jnp.sin(angles)], axis=1).reshape(6, head_dim // 2, LANES)
-
         def head_rows(w):
             return w.transpose(0, 2, 3, 1).reshape(num_layers * num_heads * head_dim, d_model)
 
@@ -753,13 +751,13 @@
                 jax.ShapeDtypeStruct((num_layers, LANES, seq_len), BF16),
                 jax.ShapeDtypeStruct((PAD, d_model), BF16),
             ),
-            in_specs=[any_spec, vmem, vmem, vmem, vmem] + [any_spec] * 7,
+            in_specs=[any_spec] + [vmem] * 5 + [any_spec] * 7,
             out_specs=(any_spec, any_spec, any_spec, vmem),
             scratch_shapes=scratch,
             compiler_params=pltpu.CompilerParams(collective_id=0, has_side_effects=True, vmem_limit_bytes=67_000_000),
             name="prefill_decode",
         )(
-            x_rows, emb, norm_attn, norm_mlp, tables,
+            x_rows, emb, norm_attn, norm_mlp, jnp.cos(angles), jnp.sin(angles),
             head_rows(w_q), head_rows(w_k), head_rows(w_v), w_o.reshape(num_layers * d_model, d_model),
             w_gate.reshape(num_layers * d_model, ff_dim), w_up.reshape(num_layers * d_model, ff_dim), w_down.reshape(num_layers * ff_dim, d_model),
         )

time: 254 us -> 255 us (level)
  Pallas kernels: 250 us -> 253 us
    pallas_call x1, Pallas kernels: 243 us -> 246 us  [local_program(): pl.pallas_call(functools.partial(main_kernel, group, head_dim, num_layers...]
where the time goes in v4:
time: 255 us; the launch traced here: 254 us
  Pallas kernels  253 us (99%)
    pallas_call x1, Pallas kernels, local_program(): pl.pallas_call(functools.partial(main_kernel, group, head_dim, num_layers...  246 us

profile of v4, /device:TPU:23, one launch (start us, length us, event | category | flops | bytes accessed | tf_op | source)
XLA Modules:
  0.0 254.4 jit_solution(11442803581637861017)
XLA Ops:
  0.7 2.3 pick_rows.1.emb_in
  3.0 0.9 multiply_sine_fusion
  3.9 245.7 %prefill_decode.1 = (bf16[256,2048]{1,0:T(8,128)(2,1)}, bf16[2,128,4096]{2,1,0:T(8,128)(2,1)}, bf16[2,128,4096]{2,1,0:T(8,128)(2,1)}, bf16[16,2048]{1,0:T(8,128)(2,1)}) custom-call(bf16[256,2048]{1,0:T(8,128)(2,1)} %x_in.1, bf16[16,2048]{1,0:T(8,128)(2,1)} %pick_rows.1.emb_in, bf16[2,2048]{1,0:T(2,128)(2,1)} %gain_attn.1, bf16[2,2048]{1,0:T(2,128)(2,1)} %gain_mlp.1, ...), custom_call_target="tpu_custom_call" | custom-call | tf_op jit(solution)/shard_map/prefill_decode/pallas_call | solution.py:746
  249.6 4.6 %place.1 = (bf16[256,2048]{1,0:T(8,128)(2,1)}, bf16[2,128,4096]{2,1,0:T(8,128)(2,1)}, bf16[2,128,4096]{2,1,0:T(8,128)(2,1)}, bf16[4,2048]{1,0:T(4,128)(2,1)}) custom-call(bf16[256,2048]{1,0:T(8,128)(2,1)} %get-tuple-element.12.x_ref, bf16[2,128,4096]{2,1,0:T(8,128)(2,1)} %get-tuple-element.13.k_ref, bf16[2,128,4096]{2,1,0:T(8,128)(2,1)} %get-tuple-element.14.v_ref, ...), custom_call_target="tpu_custom_call" | custom-call | tf_op jit(solution)/shard_map/place/pallas_call | solution.py:673
  (4 shorter events, 0.0 us)
